TPU v7x, 32 devices: a whole 2x2x4 slice. The times are simulated.
32 devices in a mesh: gx: 2 (over x), gy: 4 (over y, core), gz: 4 (over z).
Axes of the slice: x: 2, y: 2, z: 4, core: 2. Of those that a mesh axis runs over, the one named last changes fastest.
Arguments:
- flow_pops: float32 [19, 16, 32, 512], P(None, 'gx', 'gy', 'gz'), may hold values from 0 to 0.6, as said below
- heat_pops: float32 [7, 16, 32, 512], P(None, 'gx', 'gy', 'gz'), may hold values from -0.2 to 0.2
Outputs:
- flow_out: float32 [19, 16, 32, 512], P(None, 'gx', 'gy', 'gz')
- heat_out: float32 [7, 16, 32, 512], P(None, 'gx', 'gy', 'gz')
- nusselt: float32 [], replicated
Inputs may be any that keep to these rules, and one draw needn't show every extreme that they name: `flow_pops`: positive flow populations.
All inputs are finite; a program needn't handle non-finite values.
Results may differ from a plain program's by a relative error of at most 0.0001.
Values sent between devices are 32-bit elements; how exact they have to be, the bound alone decides.
No kernel may reach another device: no remote copies, remote signals or barrier semaphores. Data moves between devices by JAX's collectives and lax.ppermute only.
A program may use at most 64 MiB of HBM per device.

v0:
```python
import jax
import jax.numpy as jnp
import numpy as np
from jax import lax
from jax.sharding import PartitionSpec as P

STEPS = 3


FLOW_SET = np.array(
    [
        [0, 0, 0],
        [1, 0, 0],
        [-1, 0, 0],
        [0, 1, 0],
        [0, -1, 0],
        [0, 0, 1],
        [0, 0, -1],
        [1, 1, 0],
        [-1, -1, 0],
        [1, -1, 0],
        [-1, 1, 0],
        [1, 0, 1],
        [-1, 0, -1],
        [1, 0, -1],
        [-1, 0, 1],
        [0, 1, 1],
        [0, -1, -1],
        [0, 1, -1],
        [0, -1, 1],
    ]
)
FLOW_WEIGHT = np.array([1.0 / 3.0] + [1.0 / 18.0] * 6 + [1.0 / 36.0] * 12)
D3Q7_QUADRATURE = np.array([0.25] + [0.125] * 6)
LATTICE = np.concatenate([FLOW_SET, FLOW_SET[:7]], axis=0)
WEIGHTS = np.concatenate([FLOW_WEIGHT, D3Q7_QUADRATURE])
OPPOSITE = np.array(
    [[r for r in range(19) if (FLOW_SET[r] == -FLOW_SET[q]).all()][0] for q in range(19)]
    + [19 + [r for r in range(7) if (FLOW_SET[r] == -FLOW_SET[q]).all()][0] for q in range(7)]
)
TAU_FLOW = 0.6
TAU_HEAT = 0.7
GRAVITY_LIFT = 0.01
HOT_WALL = 0.5
COLD_WALL = -0.5
DIFFUSIVITY = (TAU_HEAT - 0.5) / 4.0


def shifted(block, axis, distance):
    devices = range(lax.axis_size(axis))
    route = [((i - distance) % len(devices), i) for i in devices]
    return lax.ppermute(block, axis, route)


def from_behind(value, axis, steps):
    count = lax.axis_size(axis)
    leading, last = (max(0, -steps), min(count, count - steps))
    return lax.ppermute(value, axis, [(source, source + steps) for source in range(leading, last)])


def stacked_subarray(values, count):
    return jnp.asarray(values, jnp.float32).reshape(count, 1, 1, 1)


def hydrodynamic_observables(momentum_populations, energy_populations):
    mass_per_site = jnp.sum(momentum_populations, axis=0)
    site_warmth = jnp.sum(energy_populations, axis=0)
    gravity_direction_push = GRAVITY_LIFT * mass_per_site * site_warmth
    speed_xaxis_component = (
        jnp.sum(stacked_subarray(FLOW_SET[:, 0], 19) * momentum_populations, axis=0) / mass_per_site
    )
    speed_yaxis_component = (
        jnp.sum(stacked_subarray(FLOW_SET[:, 1], 19) * momentum_populations, axis=0) / mass_per_site
    )
    speed_zaxis_component = (
        jnp.sum(stacked_subarray(FLOW_SET[:, 2], 19) * momentum_populations, axis=0)
        + 0.5 * gravity_direction_push
    ) / mass_per_site
    return (
        mass_per_site,
        site_warmth,
        gravity_direction_push,
        speed_xaxis_component,
        speed_yaxis_component,
        speed_zaxis_component,
    )


def collide(momentum_populations, energy_populations):
    (
        mass_per_site,
        site_warmth,
        gravity_direction_push,
        speed_xaxis_component,
        speed_yaxis_component,
        speed_zaxis_component,
    ) = hydrodynamic_observables(momentum_populations, energy_populations)
    dir_z = stacked_subarray(FLOW_SET[:, 2], 19)
    projected_onto_link = (
        stacked_subarray(FLOW_SET[:, 0], 19) * speed_xaxis_component
        + stacked_subarray(FLOW_SET[:, 1], 19) * speed_yaxis_component
        + dir_z * speed_zaxis_component
    )
    speed_sq = (
        speed_xaxis_component * speed_xaxis_component
        + speed_yaxis_component * speed_yaxis_component
        + speed_zaxis_component * speed_zaxis_component
    )
    weight = stacked_subarray(FLOW_WEIGHT, 19)
    equil = (
        weight
        * mass_per_site
        * (
            1.0
            + 3.0 * projected_onto_link
            + 4.5 * projected_onto_link * projected_onto_link
            - 1.5 * speed_sq
        )
    )
    source = (
        (1.0 - 0.5 / TAU_FLOW)
        * weight
        * (3.0 * (dir_z - speed_zaxis_component) + 9.0 * projected_onto_link * dir_z)
        * gravity_direction_push
    )
    flow_post = momentum_populations - (momentum_populations - equil) / TAU_FLOW + source
    warmth_rest_distribution = (
        stacked_subarray(D3Q7_QUADRATURE, 7) * site_warmth * (1.0 + 4.0 * projected_onto_link[:7])
    )
    heat_post = energy_populations - (energy_populations - warmth_rest_distribution) / TAU_HEAT
    return jnp.concatenate([flow_post, heat_post], axis=0)


def apply_walls(read, post, is_bottom, is_top):
    result = []
    for member in range(26):
        single = read[member]
        dir_z = int(LATTICE[member, 2])
        if dir_z != 0:
            plane = 0 if dir_z == 1 else single.shape[2] - 1
            flag = is_bottom if dir_z == 1 else is_top
            wall_temp = HOT_WALL if dir_z == 1 else COLD_WALL
            back = post[int(OPPOSITE[member])][:, :, plane]
            if member >= 19:
                back = -back + 2.0 * float(WEIGHTS[member]) * wall_temp
            single = single.at[:, :, plane].set(jnp.where(flag, back, single[:, :, plane]))
        result.append(single)
    return jnp.stack(result)


def local_flux(momentum_populations, energy_populations):
    (
        mass_per_site,
        site_warmth,
        gravity_direction_push,
        speed_xaxis_component,
        speed_yaxis_component,
        speed_zaxis_component,
    ) = hydrodynamic_observables(momentum_populations, energy_populations)
    return jnp.sum(speed_zaxis_component * site_warmth)


def rising(axis_col):
    return np.array([member for member in range(26) if int(LATTICE[member, axis_col]) == 1])


def falling(axis_col):
    return np.array([member for member in range(26) if int(LATTICE[member, axis_col]) == -1])


def last_plane(pops, axis_col):
    length = pops.shape[axis_col + 1]
    return lax.slice_in_dim(pops, length - 1, length, axis=axis_col + 1)[rising(axis_col)]


def first_plane(pops, axis_col):
    return lax.slice_in_dim(pops, 0, 1, axis=axis_col + 1)[falling(axis_col)]


def move_along(pops, axis_col, from_low, from_high):
    result = []
    low_count = 0
    high_count = 0
    length = pops.shape[axis_col + 1]
    for member in range(26):
        single = pops[member]
        moving = int(LATTICE[member, axis_col])
        if moving == 1:
            single = jnp.concatenate(
                [from_low[low_count], lax.slice_in_dim(single, 0, length - 1, axis=axis_col)],
                axis=axis_col,
            )
            low_count += 1
        elif moving == -1:
            single = jnp.concatenate(
                [lax.slice_in_dim(single, 1, length, axis=axis_col), from_high[high_count]],
                axis=axis_col,
            )
            high_count += 1
        result.append(single)
    return jnp.stack(result)


def per_device(flow_pops, heat_pops):
    size_x, size_y, size_z = (flow_pops.shape[1], flow_pops.shape[2], flow_pops.shape[3])
    is_bottom = lax.axis_index("gz") == 0
    is_top = lax.axis_index("gz") == lax.axis_size("gz") - 1
    momentum_populations, energy_populations = (flow_pops, heat_pops)
    for period in range(STEPS):
        post = collide(momentum_populations, energy_populations)
        moved = post
        low_x = shifted(last_plane(moved, 0), "gx", 1)
        high_x = shifted(first_plane(moved, 0), "gx", -1)
        moved = move_along(moved, 0, low_x, high_x)
        low_y = shifted(last_plane(moved, 1), "gy", 1)
        high_y = shifted(first_plane(moved, 1), "gy", -1)
        moved = move_along(moved, 1, low_y, high_y)
        low_z = from_behind(last_plane(moved, 2), "gz", 1)
        high_z = from_behind(first_plane(moved, 2), "gz", -1)
        read = move_along(moved, 2, low_z, high_z)
        read = apply_walls(read, post, is_bottom, is_top)
        momentum_populations, energy_populations = (read[:19], read[19:])
    total = lax.psum(local_flux(momentum_populations, energy_populations), ("gx", "gy", "gz"))
    cells = (
        size_x * size_y * size_z * lax.axis_size("gx") * lax.axis_size("gy") * lax.axis_size("gz")
    )
    height = size_z * lax.axis_size("gz")
    nusselt = 1.0 + height / (DIFFUSIVITY * (HOT_WALL - COLD_WALL)) * total / cells
    return (momentum_populations, energy_populations, nusselt)


def solution(mesh):
    placed = (P(None, "gx", "gy", "gz"), P(None, "gx", "gy", "gz"))
    return jax.shard_map(
        per_device,
        mesh=mesh,
        in_specs=placed,
        out_specs=(P(None, "gx", "gy", "gz"), P(None, "gx", "gy", "gz"), P()),
        check_vma=False,
    )
```

profile of v0, /device:TPU:0, one launch (start us, length us, event | category | flops | bytes accessed | tf_op | source)
XLA Modules:
  0.0 221.2 jit_solution(14215498760521662756)
XLA Ops:
  1.3 1.0 reduce_sum.665
  2.4 1.3 multiply_reduce_fusion.9
  6.5 3.0 %collective-permute-start = (f32[6,1,8,128]{3,2,1,0:T(8,128)S(1)}, f32[6,1,8,128]{3,2,1,0:T(8,128)S(1)}, u32[]{:S(2)}, u32[]{:S(2)}) collective-permute-start(f32[6,1,8,128]{3,2,1,0:T(8,128)S(1)} %bitcast.1389), channel_id=1, source_target_pairs={{16,0},{0,16},{17,1},{1,17},{18,2},{2,18},{19,3},{3,19},{20,4},{4,... | collective-permute-start | bytes 73736 | tf_op jit(solution)/shard_map/ppermute | solution.py:52
  19.7 1.8 collective-permute-start.3
  21.4 0.9 collective-permute-done.2
  30.6 1.3 copy.1081
  32.9 3.5 %collective-permute-start.4 = (f32[6,8,8,1]{3,2,1,0:T(8,128)S(1)}, f32[6,8,8,1]{3,2,1,0:T(8,128)S(1)}, u32[]{:S(2)}, u32[]{:S(2)}) collective-permute-start(f32[6,8,8,1]{3,2,1,0:T(8,128)S(1)} %copy.971), channel_id=1, source_target_pairs={{0,1},{1,2},{2,3},{4,5},{5,6},{6,7},{8,9},{9,10},{10,11},{12,13},{... | collective-permute-start | bytes 4616 | tf_op jit(solution)/shard_map/ppermute | solution.py:58
  36.5 1.3 copy.1082
  38.9 1.3 collective-permute-start.5
  40.2 1.4 collective-permute-done.4
  42.6 5.7 %collective-permute-done.5 = f32[6,8,8,1]{3,2,1,0:T(8,128)S(1)} collective-permute-done((f32[6,8,8,1]{3,2,1,0:T(8,128)S(1)}, f32[6,8,8,1]{3,2,1,0:T(8,128)S(1)}, u32[]{:S(2)}, u32[]{:S(2)}) %collective-permute-start.5) | collective-permute-done | bytes 1568 | tf_op jit(solution)/shard_map/ppermute | solution.py:58
  49.8 0.7 copy-done.17
  51.2 0.7 copy-done.15
  52.9 0.7 copy-done.141
  54.3 0.7 copy-done.140
  56.7 0.7 copy-done.136
  57.6 0.7 copy-done.131
  59.0 0.7 copy-done.130
  68.4 1.5 collective-permute-start.6
  73.9 1.3 collective-permute-done.7
  80.9 1.8 collective-permute-start.9
  91.2 1.3 copy.1083
  93.5 3.5 %collective-permute-start.10 = (f32[6,8,8,1]{3,2,1,0:T(8,128)S(1)}, f32[6,8,8,1]{3,2,1,0:T(8,128)S(1)}, u32[]{:S(2)}, u32[]{:S(2)}) collective-permute-start(f32[6,8,8,1]{3,2,1,0:T(8,128)S(1)} %copy.1013), channel_id=1, source_target_pairs={{0,1},{1,2},{2,3},{4,5},{5,6},{6,7},{8,9},{9,10},{10,11},{12,13},{... | collective-permute-start | bytes 4616 | tf_op jit(solution)/shard_map/ppermute | solution.py:58
  97.1 1.3 copy.1084
  99.5 1.5 collective-permute-start.11
  101.0 0.9 collective-permute-done.10
  102.9 5.6 %collective-permute-done.11 = f32[6,8,8,1]{3,2,1,0:T(8,128)S(1)} collective-permute-done((f32[6,8,8,1]{3,2,1,0:T(8,128)S(1)}, f32[6,8,8,1]{3,2,1,0:T(8,128)S(1)}, u32[]{:S(2)}, u32[]{:S(2)}) %collective-permute-start.11) | collective-permute-done | bytes 1568 | tf_op jit(solution)/shard_map/ppermute | solution.py:58
  110.6 0.7 copy-done.11
  111.4 0.7 copy-done.13
  112.2 0.7 copy-done.127
  113.1 0.7 copy-done.125
  117.8 0.7 copy-done.134
  129.9 1.5 collective-permute-start.13
  138.9 1.8 collective-permute-start.15
  147.5 1.3 copy.1085
  149.9 3.5 %collective-permute-start.16 = (f32[6,8,8,1]{3,2,1,0:T(8,128)S(1)}, f32[6,8,8,1]{3,2,1,0:T(8,128)S(1)}, u32[]{:S(2)}, u32[]{:S(2)}) collective-permute-start(f32[6,8,8,1]{3,2,1,0:T(8,128)S(1)} %copy.1053), channel_id=1, source_target_pairs={{0,1},{1,2},{2,3},{4,5},{5,6},{6,7},{8,9},{9,10},{10,11},{12,13},{... | collective-permute-start | bytes 4616 | tf_op jit(solution)/shard_map/ppermute | solution.py:58
  153.4 1.3 copy.1086
  155.8 1.3 collective-permute-start.17
  157.1 1.4 collective-permute-done.16
  159.5 5.6 %collective-permute-done.17 = f32[6,8,8,1]{3,2,1,0:T(8,128)S(1)} collective-permute-done((f32[6,8,8,1]{3,2,1,0:T(8,128)S(1)}, f32[6,8,8,1]{3,2,1,0:T(8,128)S(1)}, u32[]{:S(2)}, u32[]{:S(2)}) %collective-permute-start.17) | collective-permute-done | bytes 1568 | tf_op jit(solution)/shard_map/ppermute | solution.py:58
  167.2 0.7 copy-done.7
  168.0 0.7 copy-done.9
  168.7 0.7 copy-done.126
  171.1 0.7 copy-done.122
  172.5 0.7 copy-done.129
  173.4 0.7 copy-done.138
  175.8 0.7 copy-done.133
  181.3 38.1 %psum.7 = f32[]{:T(128)} all-reduce(f32[]{:T(128)} %multiply_reduce_fusion.10), channel_id=1, replica_groups=mesh['gx'=2,'gy'=4,'gz'=4] {'gx','gy','gz'}, use_global_device_ids=true, to_apply=%region_13.14 | all-reduce | flops 1 | bytes 8 | tf_op jit(solution)/shard_map/psum | solution.py:223
  (849 shorter events, 104.2 us)
Async XLA Ops:
  6.5 7.7 %collective-permute-start = (f32[6,1,8,128]{3,2,1,0:T(8,128)S(1)}, f32[6,1,8,128]{3,2,1,0:T(8,128)S(1)}, u32[]{:S(2)}, u32[]{:S(2)}) collective-permute-start(f32[6,1,8,128]{3,2,1,0:T(8,128)S(1)} %bitcast.1389), channel_id=1, source_target_pairs={{16,0},{0,16},{17,1},{1,17},{18,2},{2,18},{19,3},{3,19},{20,4},{4,... | collective-permute-start | bytes 73736 | tf_op jit(solution)/shard_map/ppermute | solution.py:52
  10.1 5.3 %collective-permute-start.1 = (f32[6,1,8,128]{3,2,1,0:T(8,128)S(1)}, f32[6,1,8,128]{3,2,1,0:T(8,128)S(1)}, u32[]{:S(2)}, u32[]{:S(2)}) collective-permute-start(f32[6,1,8,128]{3,2,1,0:T(8,128)S(1)} %bitcast.1388), channel_id=1, source_target_pairs={{16,0},{0,16},{17,1},{1,17},{18,2},{2,18},{19,3},{3,19},{20,4},{4,... | collective-permute-start | bytes 73736 | tf_op jit(solution)/shard_map/ppermute | solution.py:52
  11.4 11.5 %copy-start.38 = (f32[8,8,128]{2,1,0:T(8,128)}, f32[8,8,128]{2,1,0:T(8,128)S(1)}, u32[]{:S(2)}) copy-start(f32[8,8,128]{2,1,0:T(8,128)S(1)} %get-tuple-element.547) | copy-start | bytes 98308
  12.1 16.8 %copy-start.18 = (f32[7,8,128]{2,1,0:T(8,128)}, f32[7,8,128]{2,1,0:T(8,128)S(1)}, u32[]{:S(2)}) copy-start(f32[7,8,128]{2,1,0:T(8,128)S(1)} %get-tuple-element.584) | copy-start | bytes 86020
  12.1 16.8 %copy-start.20 = (f32[7,8,128]{2,1,0:T(8,128)}, f32[7,8,128]{2,1,0:T(8,128)S(1)}, u32[]{:S(2)}) copy-start(f32[7,8,128]{2,1,0:T(8,128)S(1)} %get-tuple-element.585) | copy-start | bytes 86020
  12.8 6.3 %copy-start.219 = (s32[1024]{0:T(1024)}, s32[1024]{0:T(1024)S(1)}, u32[]{:S(2)}) copy-start(s32[1024]{0:T(1024)S(1)} %get-tuple-element.816) | copy-start | bytes 12292
  13.5 10.7 %copy-start.53 = (f32[8,7,128]{2,1,0:T(8,128)}, f32[8,7,128]{2,1,0:T(8,128)S(1)}, u32[]{:S(2)}) copy-start(f32[8,7,128]{2,1,0:T(8,128)S(1)} %slice.2411) | copy-start | bytes 86020
  13.5 13.5 %copy-start.77 = (f32[8,7,128]{2,1,0:T(8,128)}, f32[8,7,128]{2,1,0:T(8,128)S(1)}, u32[]{:S(2)}) copy-start(f32[8,7,128]{2,1,0:T(8,128)S(1)} %slice.2437) | copy-start | bytes 86020
  16.8 8.0 %copy-start.16 = (f32[8,7,128]{2,1,0:T(8,128)}, f32[8,7,128]{2,1,0:T(8,128)S(1)}, u32[]{:S(2)}) copy-start(f32[8,7,128]{2,1,0:T(8,128)S(1)} %get-tuple-element.813) | copy-start | bytes 86020
  16.8 8.1 %copy-start.14 = (f32[8,7,128]{2,1,0:T(8,128)}, f32[8,7,128]{2,1,0:T(8,128)S(1)}, u32[]{:S(2)}) copy-start(f32[8,7,128]{2,1,0:T(8,128)S(1)} %get-tuple-element.812) | copy-start | bytes 86020
  19.0 3.3 %collective-permute-start.2 = (f32[6,8,1,128]{3,2,1,0:T(1,128)S(1)}, f32[6,8,1,128]{3,2,1,0:T(1,128)S(1)}, u32[]{:S(2)}, u32[]{:S(2)}) collective-permute-start(f32[6,8,1,128]{3,2,1,0:T(1,128)S(1)} %bitcast.1397), channel_id=1, source_target_pairs={{12,0},{0,4},{4,8},{8,12},{13,1},{1,5},{5,9},{9,13},{14,2},{2,6},{... | collective-permute-start | bytes 73736 | tf_op jit(solution)/shard_map/ppermute | solution.py:52
  19.7 3.9 %collective-permute-start.3 = (f32[6,8,1,128]{3,2,1,0:T(1,128)S(1)}, f32[6,8,1,128]{3,2,1,0:T(1,128)S(1)}, u32[]{:S(2)}, u32[]{:S(2)}) collective-permute-start(f32[6,8,1,128]{3,2,1,0:T(1,128)S(1)} %bitcast.1392), channel_id=1, source_target_pairs={{4,0},{8,4},{12,8},{0,12},{5,1},{9,5},{13,9},{1,13},{6,2},{10,6},{... | collective-permute-start | bytes 73736 | tf_op jit(solution)/shard_map/ppermute | solution.py:52
  32.9 8.7 %collective-permute-start.4 = (f32[6,8,8,1]{3,2,1,0:T(8,128)S(1)}, f32[6,8,8,1]{3,2,1,0:T(8,128)S(1)}, u32[]{:S(2)}, u32[]{:S(2)}) collective-permute-start(f32[6,8,8,1]{3,2,1,0:T(8,128)S(1)} %copy.971), channel_id=1, source_target_pairs={{0,1},{1,2},{2,3},{4,5},{5,6},{6,7},{8,9},{9,10},{10,11},{12,13},{... | collective-permute-start | bytes 4616 | tf_op jit(solution)/shard_map/ppermute | solution.py:58
  38.9 9.4 %collective-permute-start.5 = (f32[6,8,8,1]{3,2,1,0:T(8,128)S(1)}, f32[6,8,8,1]{3,2,1,0:T(8,128)S(1)}, u32[]{:S(2)}, u32[]{:S(2)}) collective-permute-start(f32[6,8,8,1]{3,2,1,0:T(8,128)S(1)} %copy.976), channel_id=1, source_target_pairs={{1,0},{2,1},{3,2},{5,4},{6,5},{7,6},{9,8},{10,9},{11,10},{13,12},{... | collective-permute-start | bytes 4616 | tf_op jit(solution)/shard_map/ppermute | solution.py:58
  66.0 17.4 %copy-start.36 = (f32[8,8,128]{2,1,0:T(8,128)}, f32[8,8,128]{2,1,0:T(8,128)S(1)}, u32[]{:S(2)}) copy-start(f32[8,8,128]{2,1,0:T(8,128)S(1)} %get-tuple-element.523) | copy-start | bytes 98308
  66.9 6.3 %copy-start.97 = (f32[7,8,128]{2,1,0:T(8,128)}, f32[7,8,128]{2,1,0:T(8,128)S(1)}, u32[]{:S(2)}) copy-start(f32[7,8,128]{2,1,0:T(8,128)S(1)} %get-tuple-element.534) | copy-start | bytes 86020
  66.9 8.9 %copy-start.95 = (f32[7,8,128]{2,1,0:T(8,128)}, f32[7,8,128]{2,1,0:T(8,128)S(1)}, u32[]{:S(2)}) copy-start(f32[7,8,128]{2,1,0:T(8,128)S(1)} %get-tuple-element.533) | copy-start | bytes 86020
  68.4 4.2 %collective-permute-start.6 = (f32[6,1,8,128]{3,2,1,0:T(8,128)S(1)}, f32[6,1,8,128]{3,2,1,0:T(8,128)S(1)}, u32[]{:S(2)}, u32[]{:S(2)}) collective-permute-start(f32[6,1,8,128]{3,2,1,0:T(8,128)S(1)} %bitcast.1395), channel_id=1, source_target_pairs={{16,0},{0,16},{17,1},{1,17},{18,2},{2,18},{19,3},{3,19},{20,4},{4,... | collective-permute-start | bytes 73736 | tf_op jit(solution)/shard_map/ppermute | solution.py:52
  70.6 19.0 %copy-start.22 = (f32[7,8,128]{2,1,0:T(8,128)}, f32[7,8,128]{2,1,0:T(8,128)S(1)}, u32[]{:S(2)}) copy-start(f32[7,8,128]{2,1,0:T(8,128)S(1)} %get-tuple-element.574) | copy-start | bytes 86020
  70.6 19.0 %copy-start.24 = (f32[7,8,128]{2,1,0:T(8,128)}, f32[7,8,128]{2,1,0:T(8,128)S(1)}, u32[]{:S(2)}) copy-start(f32[7,8,128]{2,1,0:T(8,128)S(1)} %get-tuple-element.575) | copy-start | bytes 86020
  71.3 3.9 %collective-permute-start.7 = (f32[6,1,8,128]{3,2,1,0:T(8,128)S(1)}, f32[6,1,8,128]{3,2,1,0:T(8,128)S(1)}, u32[]{:S(2)}, u32[]{:S(2)}) collective-permute-start(f32[6,1,8,128]{3,2,1,0:T(8,128)S(1)} %bitcast.1390), channel_id=1, source_target_pairs={{16,0},{0,16},{17,1},{1,17},{18,2},{2,18},{19,3},{3,19},{20,4},{4,... | collective-permute-start | bytes 73736 | tf_op jit(solution)/shard_map/ppermute | solution.py:52
  71.9 12.9 %copy-start.55 = (f32[8,7,128]{2,1,0:T(8,128)}, f32[8,7,128]{2,1,0:T(8,128)S(1)}, u32[]{:S(2)}) copy-start(f32[8,7,128]{2,1,0:T(8,128)S(1)} %slice.2535) | copy-start | bytes 86020
  72.0 15.7 %copy-start.79 = (f32[8,7,128]{2,1,0:T(8,128)}, f32[8,7,128]{2,1,0:T(8,128)S(1)}, u32[]{:S(2)}) copy-start(f32[8,7,128]{2,1,0:T(8,128)S(1)} %slice.2561) | copy-start | bytes 86020
  76.6 8.9 %copy-start.10 = (f32[8,7,128]{2,1,0:T(8,128)}, f32[8,7,128]{2,1,0:T(8,128)S(1)}, u32[]{:S(2)}) copy-start(f32[8,7,128]{2,1,0:T(8,128)S(1)} %fusion.52) | copy-start | bytes 86020
  76.6 8.9 %copy-start.12 = (f32[8,7,128]{2,1,0:T(8,128)}, f32[8,7,128]{2,1,0:T(8,128)S(1)}, u32[]{:S(2)}) copy-start(f32[8,7,128]{2,1,0:T(8,128)S(1)} %fusion.51) | copy-start | bytes 86020
  79.5 3.3 %collective-permute-start.8 = (f32[6,8,1,128]{3,2,1,0:T(1,128)S(1)}, f32[6,8,1,128]{3,2,1,0:T(1,128)S(1)}, u32[]{:S(2)}, u32[]{:S(2)}) collective-permute-start(f32[6,8,1,128]{3,2,1,0:T(1,128)S(1)} %bitcast.1399), channel_id=1, source_target_pairs={{12,0},{0,4},{4,8},{8,12},{13,1},{1,5},{5,9},{9,13},{14,2},{2,6},{... | collective-permute-start | bytes 73736 | tf_op jit(solution)/shard_map/ppermute | solution.py:52
  80.9 3.3 %collective-permute-start.9 = (f32[6,8,1,128]{3,2,1,0:T(1,128)S(1)}, f32[6,8,1,128]{3,2,1,0:T(1,128)S(1)}, u32[]{:S(2)}, u32[]{:S(2)}) collective-permute-start(f32[6,8,1,128]{3,2,1,0:T(1,128)S(1)} %bitcast.1393), channel_id=1, source_target_pairs={{4,0},{8,4},{12,8},{0,12},{5,1},{9,5},{13,9},{1,13},{6,2},{10,6},{... | collective-permute-start | bytes 73736 | tf_op jit(solution)/shard_map/ppermute | solution.py:52
  83.4 6.2 %copy-start.171 = (f32[8,1,128]{2,1,0:T(1,128)}, f32[8,1,128]{2,1,0:T(1,128)S(1)}, u32[]{:S(2)}) copy-start(f32[8,1,128]{2,1,0:T(1,128)S(1)} %get-tuple-element.767) | copy-start | bytes 12292
  93.5 8.4 %collective-permute-start.10 = (f32[6,8,8,1]{3,2,1,0:T(8,128)S(1)}, f32[6,8,8,1]{3,2,1,0:T(8,128)S(1)}, u32[]{:S(2)}, u32[]{:S(2)}) collective-permute-start(f32[6,8,8,1]{3,2,1,0:T(8,128)S(1)} %copy.1013), channel_id=1, source_target_pairs={{0,1},{1,2},{2,3},{4,5},{5,6},{6,7},{8,9},{9,10},{10,11},{12,13},{... | collective-permute-start | bytes 4616 | tf_op jit(solution)/shard_map/ppermute | solution.py:58
  99.5 9.0 %collective-permute-start.11 = (f32[6,8,8,1]{3,2,1,0:T(8,128)S(1)}, f32[6,8,8,1]{3,2,1,0:T(8,128)S(1)}, u32[]{:S(2)}, u32[]{:S(2)}) collective-permute-start(f32[6,8,8,1]{3,2,1,0:T(8,128)S(1)} %copy.1018), channel_id=1, source_target_pairs={{1,0},{2,1},{3,2},{5,4},{6,5},{7,6},{9,8},{10,9},{11,10},{13,12},{... | collective-permute-start | bytes 4616 | tf_op jit(solution)/shard_map/ppermute | solution.py:58
  102.0 6.5 %copy-start.105 = (f32[8,8,128]{2,1,0:T(8,128)S(1)}, f32[8,8,128]{2,1,0:T(8,128)}, u32[]{:S(2)}) copy-start(f32[8,8,128]{2,1,0:T(8,128)} %get-tuple-element.513) | copy-start | bytes 98308
  102.0 6.5 %copy-start.106 = (f32[8,8,128]{2,1,0:T(8,128)S(1)}, f32[8,8,128]{2,1,0:T(8,128)}, u32[]{:S(2)}) copy-start(f32[8,8,128]{2,1,0:T(8,128)} %get-tuple-element.514) | copy-start | bytes 98308
  126.2 14.7 %copy-start.34 = (f32[8,8,128]{2,1,0:T(8,128)}, f32[8,8,128]{2,1,0:T(8,128)S(1)}, u32[]{:S(2)}) copy-start(f32[8,8,128]{2,1,0:T(8,128)S(1)} %get-tuple-element.499) | copy-start | bytes 98308
  127.1 6.7 %copy-start.91 = (f32[7,8,128]{2,1,0:T(8,128)}, f32[7,8,128]{2,1,0:T(8,128)S(1)}, u32[]{:S(2)}) copy-start(f32[7,8,128]{2,1,0:T(8,128)S(1)} %get-tuple-element.509) | copy-start | bytes 86020
  128.6 3.9 %collective-permute-start.12 = (f32[6,1,8,128]{3,2,1,0:T(8,128)S(1)}, f32[6,1,8,128]{3,2,1,0:T(8,128)S(1)}, u32[]{:S(2)}, u32[]{:S(2)}) collective-permute-start(f32[6,1,8,128]{3,2,1,0:T(8,128)S(1)} %bitcast.1396), channel_id=1, source_target_pairs={{16,0},{0,16},{17,1},{1,17},{18,2},{2,18},{19,3},{3,19},{20,4},{4,... | collective-permute-start | bytes 73736 | tf_op jit(solution)/shard_map/ppermute | solution.py:52
  129.3 16.6 %copy-start.28 = (f32[7,8,128]{2,1,0:T(8,128)}, f32[7,8,128]{2,1,0:T(8,128)S(1)}, u32[]{:S(2)}) copy-start(f32[7,8,128]{2,1,0:T(8,128)S(1)} %get-tuple-element.566) | copy-start | bytes 86020
  129.3 16.6 %copy-start.26 = (f32[7,8,128]{2,1,0:T(8,128)}, f32[7,8,128]{2,1,0:T(8,128)S(1)}, u32[]{:S(2)}) copy-start(f32[7,8,128]{2,1,0:T(8,128)S(1)} %get-tuple-element.565) | copy-start | bytes 86020
  129.9 3.9 %collective-permute-start.13 = (f32[6,1,8,128]{3,2,1,0:T(8,128)S(1)}, f32[6,1,8,128]{3,2,1,0:T(8,128)S(1)}, u32[]{:S(2)}, u32[]{:S(2)}) collective-permute-start(f32[6,1,8,128]{3,2,1,0:T(8,128)S(1)} %bitcast.1391), channel_id=1, source_target_pairs={{16,0},{0,16},{17,1},{1,17},{18,2},{2,18},{19,3},{3,19},{20,4},{4,... | collective-permute-start | bytes 73736 | tf_op jit(solution)/shard_map/ppermute | solution.py:52
  131.5 10.8 %copy-start.51 = (f32[8,7,128]{2,1,0:T(8,128)}, f32[8,7,128]{2,1,0:T(8,128)S(1)}, u32[]{:S(2)}) copy-start(f32[8,7,128]{2,1,0:T(8,128)S(1)} %slice.2659) | copy-start | bytes 86020
  131.5 13.6 %copy-start.81 = (f32[8,7,128]{2,1,0:T(8,128)}, f32[8,7,128]{2,1,0:T(8,128)S(1)}, u32[]{:S(2)}) copy-start(f32[8,7,128]{2,1,0:T(8,128)S(1)} %slice.2685) | copy-start | bytes 86020
  134.6 8.3 %copy-start.6 = (f32[8,7,128]{2,1,0:T(8,128)}, f32[8,7,128]{2,1,0:T(8,128)S(1)}, u32[]{:S(2)}) copy-start(f32[8,7,128]{2,1,0:T(8,128)S(1)} %fusion.44) | copy-start | bytes 86020
  134.7 8.3 %copy-start.8 = (f32[8,7,128]{2,1,0:T(8,128)}, f32[8,7,128]{2,1,0:T(8,128)S(1)}, u32[]{:S(2)}) copy-start(f32[8,7,128]{2,1,0:T(8,128)S(1)} %fusion.43) | copy-start | bytes 86020
  137.6 3.3 %collective-permute-start.14 = (f32[6,8,1,128]{3,1,2,0:T(8,128)S(1)}, f32[6,8,1,128]{3,1,2,0:T(8,128)S(1)}, u32[]{:S(2)}, u32[]{:S(2)}) collective-permute-start(f32[6,8,1,128]{3,1,2,0:T(8,128)S(1)} %bitcast.1398), channel_id=1, source_target_pairs={{12,0},{0,4},{4,8},{8,12},{13,1},{1,5},{5,9},{9,13},{14,2},{2,6},{... | collective-permute-start | bytes 73736 | tf_op jit(solution)/shard_map/ppermute | solution.py:52
  138.9 3.3 %collective-permute-start.15 = (f32[6,8,1,128]{3,1,2,0:T(8,128)S(1)}, f32[6,8,1,128]{3,1,2,0:T(8,128)S(1)}, u32[]{:S(2)}, u32[]{:S(2)}) collective-permute-start(f32[6,8,1,128]{3,1,2,0:T(8,128)S(1)} %bitcast.1394), channel_id=1, source_target_pairs={{4,0},{8,4},{12,8},{0,12},{5,1},{9,5},{13,9},{1,13},{6,2},{10,6},{... | collective-permute-start | bytes 73736 | tf_op jit(solution)/shard_map/ppermute | solution.py:52
  149.9 8.7 %collective-permute-start.16 = (f32[6,8,8,1]{3,2,1,0:T(8,128)S(1)}, f32[6,8,8,1]{3,2,1,0:T(8,128)S(1)}, u32[]{:S(2)}, u32[]{:S(2)}) collective-permute-start(f32[6,8,8,1]{3,2,1,0:T(8,128)S(1)} %copy.1053), channel_id=1, source_target_pairs={{0,1},{1,2},{2,3},{4,5},{5,6},{6,7},{8,9},{9,10},{10,11},{12,13},{... | collective-permute-start | bytes 4616 | tf_op jit(solution)/shard_map/ppermute | solution.py:58
  155.8 9.3 %collective-permute-start.17 = (f32[6,8,8,1]{3,2,1,0:T(8,128)S(1)}, f32[6,8,8,1]{3,2,1,0:T(8,128)S(1)}, u32[]{:S(2)}, u32[]{:S(2)}) collective-permute-start(f32[6,8,8,1]{3,2,1,0:T(8,128)S(1)} %copy.1058), channel_id=1, source_target_pairs={{1,0},{2,1},{3,2},{5,4},{6,5},{7,6},{9,8},{10,9},{11,10},{13,12},{... | collective-permute-start | bytes 4616 | tf_op jit(solution)/shard_map/ppermute | solution.py:58
  158.6 6.5 %copy-start.103 = (f32[8,8,128]{2,1,0:T(8,128)S(1)}, f32[8,8,128]{2,1,0:T(8,128)}, u32[]{:S(2)}) copy-start(f32[8,8,128]{2,1,0:T(8,128)} %get-tuple-element.489) | copy-start | bytes 98308
  158.6 6.5 %copy-start.104 = (f32[8,8,128]{2,1,0:T(8,128)S(1)}, f32[8,8,128]{2,1,0:T(8,128)}, u32[]{:S(2)}) copy-start(f32[8,8,128]{2,1,0:T(8,128)} %get-tuple-element.490) | copy-start | bytes 98308
  (212 other events, 379.5 us)
where the time goes:
time: 225 us; the launch traced here: 221 us
  local copies, waits for them, and re-layouts  93.5 us (42%)
  blocking collectives  38.1 us (17%)
  other arithmetic  31 us (14%)
  starting transfers between devices  27.9 us (12%)
  waiting for transfers between devices  24.3 us (11%)
  between operations  6.25 us (3%)
    unnamed x531, local copies, waits for them, and re-layouts  44.6 us
    psum x1, blocking collectives, per_device(): lax.psum(local_flux(momentum_populations, energy_populations), ('gx', 'gy...  38.1 us
    ppermute x6, waiting for transfers between devices, from_behind(): lax.ppermute(value, axis, [(source, source + steps) for source in range(l...  20.5 us
    ppermute x6, starting transfers between devices, from_behind(): lax.ppermute(value, axis, [(source, source + steps) for source in range(l...  14.5 us
    ppermute x12, starting transfers between devices, shifted(): return lax.ppermute(block, axis, route)  13.5 us
    scatter x36, local copies, waits for them, and re-layouts, apply_walls(): single.at[:, :, plane].set(jnp.where(flag, back, single[:, :, plane]))  12 us
    unnamed x102, other arithmetic  8.25 us
    concatenate x16, other arithmetic, move_along(): jnp.concatenate([from_low[low_count], lax.slice_in_dim(single, 0, length...  7.24 us
  transfers between devices with their start and end apart: 18, of which 14 were waited for; matrix products, arithmetic and copies ran while one was open for 11% of the time, Pallas kernels for 0%

commit v1 on v0

v1 whole, which is shorter than its diff:
```python
import functools

import jax
import jax.numpy as jnp
import numpy as np
from jax import lax
from jax.experimental import pallas as pl
from jax.experimental.pallas import tpu as pltpu
from jax.sharding import PartitionSpec as P

STEPS = 3
TAU_FLOW = 0.6
TAU_HEAT = 0.7
GRAVITY_LIFT = 0.01
HOT_WALL = 0.5
COLD_WALL = -0.5
DIFFUSIVITY = (TAU_HEAT - 0.5) / 4.0

FLOW_SET = [
    (0, 0, 0),
    (1, 0, 0),
    (-1, 0, 0),
    (0, 1, 0),
    (0, -1, 0),
    (0, 0, 1),
    (0, 0, -1),
    (1, 1, 0),
    (-1, -1, 0),
    (1, -1, 0),
    (-1, 1, 0),
    (1, 0, 1),
    (-1, 0, -1),
    (1, 0, -1),
    (-1, 0, 1),
    (0, 1, 1),
    (0, -1, -1),
    (0, 1, -1),
    (0, -1, 1),
]
LATTICE = FLOW_SET + FLOW_SET[:7]
COUNT = len(LATTICE)
NFLOW = len(FLOW_SET)
OPPOSITE = [
    (0 if q < NFLOW else NFLOW) + FLOW_SET.index(tuple(-c for c in LATTICE[q])) for q in range(COUNT)
]
HEAT_WEIGHT = [0.25] + [0.125] * 6
MOVING = {
    (axis, sign): [q for q in range(COUNT) if LATTICE[q][axis] == sign]
    for axis in range(3)
    for sign in (1, -1)
}
FACE = len(MOVING[0, 1])
SLOT = 8


def lanes_of(shape):
    return lax.broadcasted_iota(jnp.int32, shape, 1)


def rows_of(shape):
    return lax.broadcasted_iota(jnp.int32, shape, 0)


def roll(tile, amount, axis):
    size = tile.shape[axis]
    amount = amount % size
    return tile if amount == 0 else pltpu.roll(tile, amount, axis)


def pack(tiles):
    lane = lanes_of(tiles[0].shape)
    packed = None
    for slot, tile in enumerate(tiles):
        tile = roll(tile, STEPS + SLOT * slot, 1)
        packed = tile if packed is None else jnp.where(lane >= SLOT * slot, tile, packed)
    return packed


def unpack(packed, slot):
    return roll(packed, -(STEPS + SLOT * slot), 1)


def moments(f):
    rho = functools.reduce(lambda a, b: a + b, f[:NFLOW])
    temp = functools.reduce(lambda a, b: a + b, f[NFLOW:])
    diff = {q: f[q] - f[q + 1] for q in range(1, NFLOW, 2)}
    flux = []
    for axis in range(3):
        total = None
        for q in range(1, NFLOW, 2):
            c = LATTICE[q][axis]
            if c:
                assert total is not None or c == 1
                total = diff[q] if total is None else total + diff[q] if c == 1 else total - diff[q]
        flux.append(total)
    push = GRAVITY_LIFT * rho * temp
    inverse = 1.0 / rho
    return rho, temp, push, flux[0] * inverse, flux[1] * inverse, (flux[2] + 0.5 * push) * inverse


def collide(f):
    rho, temp, push, ux, uy, uz = moments(f)
    u = (ux, uy, uz)
    keep = 1.0 - 1.0 / TAU_FLOW
    scale = rho * (1.0 / TAU_FLOW / 36.0)
    source = push * ((1.0 - 0.5 / TAU_FLOW) / 36.0)
    base = scale * (1.0 - 1.5 * (ux * ux + uy * uy + uz * uz)) - 3.0 * source * uz
    linear, square = 3.0 * scale, 4.5 * scale
    push1, push2 = 3.0 * source, 9.0 * source
    out = [None] * COUNT
    out[0] = keep * f[0] + 12.0 * base
    for q in range(1, NFLOW, 2):
        c = LATTICE[q]
        along = None
        for axis in range(3):
            if c[axis]:
                along = u[axis] if along is None else along + u[axis] if c[axis] == 1 else along - u[axis]
        inner = square * along
        odd = linear * along
        if c[2] == 1:
            inner, odd = inner + push2, odd + push1
        elif c[2] == -1:
            inner, odd = inner - push2, odd - push1
        even = base + inner * along
        if q < 7:
            even, odd = 2.0 * even, 2.0 * odd
        out[q] = keep * f[q] + (even + odd)
        out[q + 1] = keep * f[q + 1] + (even - odd)
    keep = 1.0 - 1.0 / TAU_HEAT
    out[NFLOW] = keep * f[NFLOW] + (HEAT_WEIGHT[0] / TAU_HEAT) * temp
    rest = (HEAT_WEIGHT[1] / TAU_HEAT) * temp
    for axis in range(3):
        q = NFLOW + 1 + 2 * axis
        drift = 4.0 * rest * u[axis]
        out[q] = keep * f[q] + (rest + drift)
        out[q + 1] = keep * f[q + 1] + (rest - drift)
    return out


def send(outs, up, down, odd):
    if len(outs) == 1:
        for j, tile in enumerate(up + down):
            outs[0][j] = tile
    else:
        for j in range(len(up)):
            outs[0][j] = jnp.where(odd, down[j], up[j])
            outs[1][j] = jnp.where(odd, up[j], down[j])


def received(ins, odd, count):
    if len(ins) == 1:
        return (lambda j: ins[0][j]), (lambda j: ins[0][count + j])
    low = lambda j: jnp.where(odd, ins[0][j], ins[1][j])
    high = lambda j: jnp.where(odd, ins[1][j], ins[0][j])
    return low, high


def swap(buffers, axis, size, periodic):
    if size == 1:
        return list(buffers)
    first = [(i, i + 1) for i in range(0, size - 1, 2)]
    second = [(i, i + 1) for i in range(1, size - 1, 2)] + ([(size - 1, 0)] if periodic else [])
    both = lambda pairs: [p for a, b in pairs for p in ((a, b), (b, a))]
    if len(buffers) == 1:
        return [lax.ppermute(buffers[0], axis, both(first))]
    return [lax.ppermute(b, axis, both(pairs)) for b, pairs in zip(buffers, (first, second))]


def face_x(post, halo, extent):
    up = [post(q, extent - 1) for q in MOVING[0, 1]]
    down = [post(q, 0) for q in MOVING[0, -1]]
    up.append(pack([halo(q, extent - 1) for q in MOVING[0, 1]]))
    down.append(pack([halo(q, 0) for q in MOVING[0, -1]]))
    return up, down


def call(kernel, ins, outs, flops, scratch=()):
    vmem = pl.BlockSpec(memory_space=pltpu.VMEM)
    smem = pl.BlockSpec(memory_space=pltpu.SMEM)
    return pl.pallas_call(
        kernel,
        out_shape=[jax.ShapeDtypeStruct(s, jnp.float32) for s in outs],
        in_specs=[smem] + [vmem] * (len(ins) - 1),
        out_specs=[vmem] * len(outs),
        scratch_shapes=[pltpu.VMEM(s, jnp.float32) for s in scratch],
        compiler_params=pltpu.CompilerParams(vmem_limit_bytes=12 * 2**20),
        cost_estimate=pl.CostEstimate(flops=flops, bytes_accessed=flops // 8, transcendentals=0),
    )(*ins)


def per_device(sizes, flow, heat):
    X, Y, Z = flow.shape[1:]
    assert Z >= 2 * STEPS and Z % SLOT == 0
    slots = Z // SLOT
    ztiles = -(-COUNT * X // slots)
    nx, ny, nz = (sizes[a] for a in ("gx", "gy", "gz"))
    assert all(n == 1 or n % 2 == 0 for n in (nx, ny, nz))
    tile = (Y, Z)
    bx = 1 if nx <= 2 else 2
    by = 1 if ny <= 2 else 2
    xshape = (2 * (FACE + 1) // bx, Y, Z)
    yshape = (2 * (FACE + 1) // by, X, Z)
    big = (COUNT, X, Y, Z)
    ix, iy, iz = (lax.axis_index(a) for a in ("gx", "gy", "gz"))
    info = jnp.stack([ix % 2, iy % 2, iz % 2, iz == 0, iz == nz - 1]).astype(jnp.int32)
    work = COUNT * X * Y * Z * 10

    def whole(flow_ref, heat_ref):
        return lambda q, x: flow_ref[q, x] if q < NFLOW else heat_ref[q - NFLOW, x]

    def pack_z(info_ref, flow_ref, heat_ref, out_ref):
        get = whole(flow_ref, heat_ref)
        entries = [(q, x) for q in range(COUNT) for x in range(X)]
        for t in range(ztiles):
            out_ref[t] = pack([get(q, x) for q, x in entries[t * slots : (t + 1) * slots]])

    def first_main(info_ref, flow_ref, heat_ref, post_ref):
        get = whole(flow_ref, heat_ref)
        for x in range(X):
            for q, value in enumerate(collide([get(q, x) for q in range(COUNT)])):
                post_ref[q, x] = value

    def first_halo(info_ref, za_ref, zb_ref, post_ref, halo_ref, *x_refs):
        merged = x_refs[-1]
        odd_z = info_ref[2] == 1
        inner = lanes_of(tile) % SLOT < STEPS
        for t in range(ztiles):
            a, b = za_ref[t], zb_ref[t]
            low, high = jnp.where(odd_z, a, b), jnp.where(odd_z, b, a)
            merged[t] = jnp.where(inner, low, high)
        for x in range(X):
            f = []
            for q in range(COUNT):
                t, slot = divmod(q * X + x, slots)
                f.append(unpack(merged[t], slot))
            for q, value in enumerate(collide(f)):
                halo_ref[q, x] = value
        up, down = face_x(lambda q, x: post_ref[q, x], lambda q, x: halo_ref[q, x], X)
        send(x_refs[:-1], up, down, info_ref[0] == 1)

    def pack_y(info_ref, post_ref, halo_ref, *refs):
        x_refs, y_refs = refs[:bx], refs[bx:]
        x_low, x_high = received(x_refs, info_ref[0] == 1, FACE + 1)
        sub = rows_of((X, Z))

        def rows(q, row):
            main, halo = post_ref[q, :, row, :], halo_ref[q, :, row, :]
            cx = LATTICE[q][0]
            if cx:
                source, members = (x_low, MOVING[0, 1]) if cx == 1 else (x_high, MOVING[0, -1])
                j = members.index(q)
                edge = sub == (0 if cx == 1 else X - 1)
                at_main = source(j)[row : row + 1, :]
                at_halo = unpack(source(FACE)[row : row + 1, :], j)
                main = jnp.where(edge, at_main, roll(main, cx, 0))
                halo = jnp.where(edge, at_halo, roll(halo, cx, 0))
            return main, halo

        ways = []
        for sign, row in ((1, Y - 1), (-1, 0)):
            pairs = [rows(q, row) for q in MOVING[1, sign]]
            ways.append([m for m, _ in pairs] + [pack([h for _, h in pairs])])
        send(y_refs, ways[0], ways[1], info_ref[1] == 1)

    def stream(info_ref, post_ref, halo_ref, x_refs, y_refs, yh_ref, use):
        x_low, x_high = received(x_refs, info_ref[0] == 1, FACE + 1)
        y_low, y_high = received(y_refs, info_ref[1] == 1, FACE + 1)
        lane, sub = lanes_of(tile), rows_of(tile)
        first, last = lane == 0, lane == Z - 1
        at_bottom = first & (info_ref[3] == 1)
        at_top = last & (info_ref[4] == 1)
        for j in range(FACE):
            yh_ref[j] = unpack(y_low(FACE), j)
            yh_ref[FACE + j] = unpack(y_high(FACE), j)
            yh_ref[2 * FACE + j] = y_low(j)
            yh_ref[3 * FACE + j] = y_high(j)
        for x in range(X):
            mains, halos = [], []
            for q in range(COUNT):
                cx, cy, cz = LATTICE[q]
                if 0 <= x - cx < X:
                    main, halo = post_ref[q, x - cx], halo_ref[q, x - cx]
                else:
                    source, members = (x_low, MOVING[0, 1]) if cx == 1 else (x_high, MOVING[0, -1])
                    j = members.index(q)
                    main, halo = source(j), unpack(source(FACE), j)
                if cy:
                    j = MOVING[1, cy].index(q) + (0 if cy == 1 else FACE)
                    edge = sub == (0 if cy == 1 else Y - 1)
                    main = jnp.where(edge, yh_ref[2 * FACE + j, x : x + 1, :], roll(main, cy, 0))
                    halo = jnp.where(edge, yh_ref[j, x : x + 1, :], roll(halo, cy, 0))
                if cz:
                    edge, wall = (first, at_bottom) if cz == 1 else (last, at_top)
                    main, halo = roll(main, cz, 1), roll(halo, cz, 1)
                    main, halo = jnp.where(edge, halo, main), jnp.where(edge, main, halo)
                    back = post_ref[OPPOSITE[q], x]
                    if q >= NFLOW:
                        at_wall = HOT_WALL if cz == 1 else COLD_WALL
                        back = 2.0 * HEAT_WEIGHT[q - NFLOW] * at_wall - back
                    main = jnp.where(wall, back, main)
                mains.append(main)
                halos.append(halo)
            use(x, mains, halos)

    def middle(info_ref, post_ref, halo_ref, *refs):
        x_refs, y_refs, refs = refs[:bx], refs[bx : bx + by], refs[bx + by :]
        new_ref, new_halo_ref, xo_refs, yh_ref = refs[0], refs[1], refs[2:-1], refs[-1]

        def use(x, mains, halos):
            for q, value in enumerate(halos):
                new_halo_ref[q, x] = value
            for q, value in enumerate(collide(mains)):
                new_ref[q, x] = value
            for q, value in enumerate(collide([new_halo_ref[q, x] for q in range(COUNT)])):
                new_halo_ref[q, x] = value

        stream(info_ref, post_ref, halo_ref, x_refs, y_refs, yh_ref, use)
        up, down = face_x(lambda q, x: new_ref[q, x], lambda q, x: new_halo_ref[q, x], X)
        send(xo_refs, up, down, info_ref[0] == 1)

    devices = nx * ny * nz

    def final(info_ref, post_ref, halo_ref, *refs):
        x_refs, y_refs, refs = refs[:bx], refs[bx : bx + by], refs[bx + by :]
        flow_ref, heat_ref, part_ref, yh_ref = refs
        total = [jnp.zeros(tile, jnp.float32)]

        def use(x, mains, halos):
            for q, value in enumerate(mains):
                if q < NFLOW:
                    flow_ref[q, x] = value
                else:
                    heat_ref[q - NFLOW, x] = value
            _, temp, _, _, _, uz = moments(mains)
            total[0] = total[0] + uz * temp

        stream(info_ref, post_ref, halo_ref, x_refs, y_refs, yh_ref, use)
        part = jnp.sum(total[0], axis=0, keepdims=True)
        part_ref[...] = jnp.broadcast_to(part[None], part_ref.shape)

    (zpack,) = call(pack_z, (info, flow, heat), [(ztiles, Y, Z)], work)
    za, zb = swap([zpack, zpack], "gz", nz, False)
    (post,) = call(first_main, (info, flow, heat), [big], 20 * work)
    post_halo, *xs = call(
        first_halo, (info, za, zb, post), [big] + [xshape] * bx, 20 * work, [(ztiles, Y, Z)]
    )
    for step in range(STEPS):
        xs = swap(xs, "gx", nx, True)
        ys = call(pack_y, (info, post, post_halo, *xs), [yshape] * by, work)
        ys = swap(ys, "gy", ny, True)
        ins = (info, post, post_halo, *xs, *ys)
        scratch = [(4 * FACE, X, Z)]
        if step < STEPS - 1:
            post, post_halo, *xs = call(middle, ins, [big, big] + [xshape] * bx, 20 * work, scratch)
        else:
            flow, heat, parts = call(
                final, ins, [flow.shape, heat.shape, (devices, 1, Z)], 20 * work, scratch
            )
    parts = lax.all_to_all(parts, ("gx", "gy", "gz"), 0, 0, tiled=True)
    cells = X * Y * Z * devices
    factor = Z * nz / (DIFFUSIVITY * (HOT_WALL - COLD_WALL)) / cells
    nusselt = 1.0 + factor * jnp.sum(parts)
    return flow, heat, nusselt


def solution(mesh):
    placed = P(None, "gx", "gy", "gz")
    return jax.shard_map(
        functools.partial(per_device, dict(mesh.shape)),
        mesh=mesh,
        in_specs=(placed, placed),
        out_specs=(placed, placed, P()),
        check_vma=False,
    )
```

time: 225 us -> 56.9 us (0.25); the launches traced: 221 us -> 56.7 us
  local copies, waits for them, and re-layouts: 93.5 us -> 2.1 us
  other arithmetic: 31 us -> 0.63 us
  blocking collectives: 38.1 us -> 11.3 us
  starting transfers between devices: 27.9 us -> 16.4 us
  waiting for transfers between devices: 24.3 us -> 14.7 us
  Pallas kernels: 0 us -> 9.04 us
  between operations: 6.25 us -> 2.55 us
    unnamed x531 -> x4, local copies, waits for them, and re-layouts: 44.6 us -> 2.01 us
    psum x1 -> x0, blocking collectives: 38.1 us -> none  [per_device(): lax.psum(local_flux(momentum_populations, energy_populations), ('gx', 'gy...]
    slice x44 -> x0, local copies, waits for them, and re-layouts: 17.4 us -> none  [the longest x9 5.14 us: first_plane(): return lax.slice_in_dim(pops, 0, 1, axis=axis_col + 1)[falling(axis_col)]]
    gather x24 -> x0, local copies, waits for them, and re-layouts: 13.9 us -> none  [the longest x12 6.94 us: last_plane(): lax.slice_in_dim(pops, length - 1, length, axis=axis_col + 1)]
    concatenate x33 -> x0, other arithmetic: 12.6 us -> none  [the longest x16 7.24 us: move_along(): jnp.concatenate([from_low[low_count], lax.slice_in_dim(single, 0, length...]
    scatter x36 -> x0, local copies, waits for them, and re-layouts: 12 us -> none  [apply_walls(): single.at[:, :, plane].set(jnp.where(flag, back, single[:, :, plane]))]
    ppermute x18 -> x11, starting transfers between devices: 27.9 us -> 16.4 us  [the longest x8 11.7 us: swap(): lax.ppermute(b, axis, both(pairs))]
    all_to_all x0 -> x1, blocking collectives: none -> 11.3 us  [per_device(): parts = lax.all_to_all(parts, ('gx', 'gy', 'gz'), 0, 0, tiled=True)]
  transfers between devices with their start and end apart: 18 -> 11, of which waited for: 14 -> 7; matrix products, arithmetic and copies ran while one was open for 11% -> 0% of each run, Pallas kernels for 0% -> 2%
where the time goes in v1:
time: 56.9 us; the launch traced here: 56.7 us
  starting transfers between devices  16.4 us (29%)
  waiting for transfers between devices  14.7 us (26%)
  blocking collectives  11.3 us (20%)
  Pallas kernels  9.04 us (16%)
  between operations  2.55 us (4%)
  local copies, waits for them, and re-layouts  2.1 us (4%)
  other arithmetic  0.63 us (1%)
    ppermute x8, starting transfers between devices, swap(): lax.ppermute(b, axis, both(pairs))  11.7 us
    all_to_all x1, blocking collectives, per_device(): parts = lax.all_to_all(parts, ('gx', 'gy', 'gz'), 0, 0, tiled=True)  11.3 us
    pallas_call x9, Pallas kernels, call(): pl.pallas_call(kernel, out_shape=[jax.ShapeDtypeStruct(s, jnp.float32) fo...  9.04 us
    ppermute x3, waiting for transfers between devices, swap(): return [lax.ppermute(buffers[0], axis, both(first))]  8.21 us
    ppermute x8, waiting for transfers between devices, swap(): lax.ppermute(b, axis, both(pairs))  6.45 us
    ppermute x3, starting transfers between devices, swap(): return [lax.ppermute(buffers[0], axis, both(first))]  4.67 us
    unnamed x4, local copies, waits for them, and re-layouts  2.01 us
  transfers between devices with their start and end apart: 11, of which 7 were waited for; matrix products, arithmetic and copies ran while one was open for 0% of the time, Pallas kernels for 2%

profile of v1, /device:TPU:0, one launch (start us, length us, event | category | flops | bytes accessed | tf_op | source)
XLA Modules:
  0.0 56.7 jit_solution(11203103274068639709)
XLA Ops:
  0.7 0.1 stack.31.info_ref
  0.7 0.0 copy-start
  0.7 1.1 %copy-done = f32[19,8,8,128]{3,2,1,0:T(8,128)S(1)} copy-done((f32[19,8,8,128]{3,2,1,0:T(8,128)S(1)}, f32[19,8,8,128]{3,2,1,0:T(8,128)}, u32[]{:S(2)}) %copy-start) | copy-done | bytes 622616
  1.8 0.0 copy-start.1
  1.8 0.9 %copy-done.1 = f32[7,8,8,128]{3,2,1,0:T(8,128)S(1)} copy-done((f32[7,8,8,128]{3,2,1,0:T(8,128)S(1)}, f32[7,8,8,128]{3,2,1,0:T(8,128)}, u32[]{:S(2)}) %copy-start.1) | copy-done | bytes 229400
  2.8 0.8 %shard_map.50 = f32[13,8,128]{2,1,0:T(8,128)S(1)} custom-call(s32[5]{0:T(128)S(1)} %stack.31.info_ref, f32[19,8,8,128]{3,2,1,0:T(8,128)S(1)} %copy-done, f32[7,8,8,128]{3,2,1,0:T(8,128)S(1)} %copy-done.1), custom_call_target="tpu_custom_call" | custom-call | flops 2129920 | bytes 266240 | tf_op jit(solution)/shard_map/pallas_call | solution.py:180
  3.6 0.7 %collective-permute-start.1 = (f32[13,8,128]{2,1,0:T(8,128)S(1)}, f32[13,8,128]{2,1,0:T(8,128)S(1)}, u32[]{:S(2)}, u32[]{:S(2)}) collective-permute-start(f32[13,8,128]{2,1,0:T(8,128)S(1)} %shard_map.50), channel_id=1, source_target_pairs={{1,2},{2,1},{5,6},{6,5},{9,10},{10,9},{13,14},{14,13},{17,18},{18,... | collective-permute-start | bytes 159752 | tf_op jit(solution)/shard_map/ppermute | solution.py:166
  4.3 5.9 %collective-permute-start = (f32[13,8,128]{2,1,0:T(8,128)S(1)}, f32[13,8,128]{2,1,0:T(8,128)S(1)}, u32[]{:S(2)}, u32[]{:S(2)}) collective-permute-start(f32[13,8,128]{2,1,0:T(8,128)S(1)} %shard_map.50), channel_id=1, source_target_pairs={{0,1},{1,0},{2,3},{3,2},{4,5},{5,4},{6,7},{7,6},{8,9},{9,8},{10,11... | collective-permute-start | bytes 159752 | tf_op jit(solution)/shard_map/ppermute | solution.py:166
  10.2 0.9 %shard_map.49.post_ref = f32[26,8,8,128]{3,2,1,0:T(8,128)S(1)} custom-call(s32[5]{0:T(128)S(1)} %stack.31.info_ref, f32[19,8,8,128]{3,2,1,0:T(8,128)S(1)} %copy-done, f32[7,8,8,128]{3,2,1,0:T(8,128)S(1)} %copy-done.1), custom_call_target="tpu_custom_call" | custom-call | flops 42598400 | bytes 5324800 | tf_op jit(solution)/shard_map/pallas_call | solution.py:180
  11.1 0.0 collective-permute-done.1.zb_ref
  11.1 1.2 %collective-permute-done.za_ref = f32[13,8,128]{2,1,0:T(8,128)S(1)} collective-permute-done((f32[13,8,128]{2,1,0:T(8,128)S(1)}, f32[13,8,128]{2,1,0:T(8,128)S(1)}, u32[]{:S(2)}, u32[]{:S(2)}) %collective-permute-start) | collective-permute-done | bytes 53280 | tf_op jit(solution)/shard_map/ppermute | solution.py:166
  12.3 0.9 %shard_map.51 = (f32[26,8,8,128]{3,2,1,0:T(8,128)S(1)}, f32[14,8,128]{2,1,0:T(8,128)S(1)}) custom-call(s32[5]{0:T(128)S(1)} %stack.31.info_ref, f32[13,8,128]{2,1,0:T(8,128)S(1)} %collective-permute-done.za_ref, f32[13,8,128]{2,1,0:T(8,128)S(1)} %collective-permute-done.1.zb_ref, f32[26,8,8,128]{3,2,1,0:T(8,128)S(1)} %shard_map.49.post_ref), custom_call_target="tpu_custom_call" | custom-call | flops 42598400 | bytes 5324800 | tf_op jit(solution)/shard_map/pallas_call | solution.py:180
  13.2 1.6 %collective-permute-start.2 = (f32[14,8,128]{2,1,0:T(8,128)S(1)}, f32[14,8,128]{2,1,0:T(8,128)S(1)}, u32[]{:S(2)}, u32[]{:S(2)}) collective-permute-start(f32[14,8,128]{2,1,0:T(8,128)S(1)} %get-tuple-element.21), channel_id=1, source_target_pairs={{0,16},{16,0},{1,17},{17,1},{2,18},{18,2},{3,19},{19,3},{4,20},{20... | collective-permute-start | bytes 172040 | tf_op jit(solution)/shard_map/ppermute | solution.py:165
  14.8 2.7 %collective-permute-done.2.refs_0_ = f32[14,8,128]{2,1,0:T(8,128)S(1)} collective-permute-done((f32[14,8,128]{2,1,0:T(8,128)S(1)}, f32[14,8,128]{2,1,0:T(8,128)S(1)}, u32[]{:S(2)}, u32[]{:S(2)}) %collective-permute-start.2) | collective-permute-done | bytes 57376 | tf_op jit(solution)/shard_map/ppermute | solution.py:165
  17.5 0.7 %shard_map.52 = (f32[7,8,128]{2,1,0:T(8,128)S(1)}, f32[7,8,128]{2,1,0:T(8,128)S(1)}) custom-call(s32[5]{0:T(128)S(1)} %stack.31.info_ref, f32[26,8,8,128]{3,2,1,0:T(8,128)S(1)} %shard_map.49.post_ref, f32[26,8,8,128]{3,2,1,0:T(8,128)S(1)} %get-tuple-element.20.halo_ref, f32[14,8,128]{2,1,0:T(8,128)S(1)} %collective-permute-done.2.refs_0_), custom_call_target="tpu_custom_call" | custom-call | flops 2129920 | bytes 266240 | tf_op jit(solution)/shard_map/pallas_call | solution.py:180
  18.2 0.1 collective-permute-start.3
  18.2 1.6 %collective-permute-start.4 = (f32[7,8,128]{2,1,0:T(8,128)S(1)}, f32[7,8,128]{2,1,0:T(8,128)S(1)}, u32[]{:S(2)}, u32[]{:S(2)}) collective-permute-start(f32[7,8,128]{2,1,0:T(8,128)S(1)} %get-tuple-element.23), channel_id=1, source_target_pairs={{4,8},{8,4},{12,0},{0,12},{5,9},{9,5},{13,1},{1,13},{6,10},{10,6},... | collective-permute-start | bytes 86024 | tf_op jit(solution)/shard_map/ppermute | solution.py:166
  19.9 0.0 collective-permute-done.3.refs_1_
  19.9 1.7 %collective-permute-done.4.refs_2_ = f32[7,8,128]{2,1,0:T(8,128)S(1)} collective-permute-done((f32[7,8,128]{2,1,0:T(8,128)S(1)}, f32[7,8,128]{2,1,0:T(8,128)S(1)}, u32[]{:S(2)}, u32[]{:S(2)}) %collective-permute-start.4) | collective-permute-done | bytes 28704 | tf_op jit(solution)/shard_map/ppermute | solution.py:166
  21.6 1.3 %shard_map.53 = (f32[26,8,8,128]{3,2,1,0:T(8,128)S(1)}, f32[26,8,8,128]{3,2,1,0:T(8,128)S(1)}, f32[14,8,128]{2,1,0:T(8,128)S(1)}) custom-call(s32[5]{0:T(128)S(1)} %stack.31.info_ref, f32[26,8,8,128]{3,2,1,0:T(8,128)S(1)} %shard_map.49.post_ref, f32[26,8,8,128]{3,2,1,0:T(8,128)S(1)} %get-tuple-element.20.halo_ref, ...), custom_call_target="tpu_custom_call" | custom-call | flops 42598400 | bytes 5324800 | tf_op jit(solution)/shard_map/pallas_call | solution.py:180
  23.0 1.6 %collective-permute-start.5 = (f32[14,8,128]{2,1,0:T(8,128)S(1)}, f32[14,8,128]{2,1,0:T(8,128)S(1)}, u32[]{:S(2)}, u32[]{:S(2)}) collective-permute-start(f32[14,8,128]{2,1,0:T(8,128)S(1)} %get-tuple-element.26), channel_id=1, source_target_pairs={{0,16},{16,0},{1,17},{17,1},{2,18},{18,2},{3,19},{19,3},{4,20},{20... | collective-permute-start | bytes 172040 | tf_op jit(solution)/shard_map/ppermute | solution.py:165
  24.5 2.8 %collective-permute-done.5.refs_0_ = f32[14,8,128]{2,1,0:T(8,128)S(1)} collective-permute-done((f32[14,8,128]{2,1,0:T(8,128)S(1)}, f32[14,8,128]{2,1,0:T(8,128)S(1)}, u32[]{:S(2)}, u32[]{:S(2)}) %collective-permute-start.5) | collective-permute-done | bytes 57376 | tf_op jit(solution)/shard_map/ppermute | solution.py:165
  27.3 0.7 %shard_map.54 = (f32[7,8,128]{2,1,0:T(8,128)S(1)}, f32[7,8,128]{2,1,0:T(8,128)S(1)}) custom-call(s32[5]{0:T(128)S(1)} %stack.31.info_ref, f32[26,8,8,128]{3,2,1,0:T(8,128)S(1)} %get-tuple-element.24.post_ref, f32[26,8,8,128]{3,2,1,0:T(8,128)S(1)} %get-tuple-element.25.halo_ref, f32[14,8,128]{2,1,0:T(8,128)S(1)} %collective-permute-done.5.refs_0_), custom_call_target="tpu_custom_call" | custom-call | flops 2129920 | bytes 266240 | tf_op jit(solution)/shard_map/pallas_call | solution.py:180
  27.9 0.1 collective-permute-start.6
  28.0 1.6 %collective-permute-start.7 = (f32[7,8,128]{2,1,0:T(8,128)S(1)}, f32[7,8,128]{2,1,0:T(8,128)S(1)}, u32[]{:S(2)}, u32[]{:S(2)}) collective-permute-start(f32[7,8,128]{2,1,0:T(8,128)S(1)} %get-tuple-element.28), channel_id=1, source_target_pairs={{4,8},{8,4},{12,0},{0,12},{5,9},{9,5},{13,1},{1,13},{6,10},{10,6},... | collective-permute-start | bytes 86024 | tf_op jit(solution)/shard_map/ppermute | solution.py:166
  29.6 0.0 collective-permute-done.6.refs_1_
  29.6 1.7 %collective-permute-done.7.refs_2_ = f32[7,8,128]{2,1,0:T(8,128)S(1)} collective-permute-done((f32[7,8,128]{2,1,0:T(8,128)S(1)}, f32[7,8,128]{2,1,0:T(8,128)S(1)}, u32[]{:S(2)}, u32[]{:S(2)}) %collective-permute-start.7) | collective-permute-done | bytes 28704 | tf_op jit(solution)/shard_map/ppermute | solution.py:166
  31.4 1.3 %shard_map.55 = (f32[26,8,8,128]{3,2,1,0:T(8,128)S(1)}, f32[26,8,8,128]{3,2,1,0:T(8,128)S(1)}, f32[14,8,128]{2,1,0:T(8,128)S(1)}) custom-call(s32[5]{0:T(128)S(1)} %stack.31.info_ref, f32[26,8,8,128]{3,2,1,0:T(8,128)S(1)} %get-tuple-element.24.post_ref, f32[26,8,8,128]{3,2,1,0:T(8,128)S(1)} %get-tuple-element.25.halo_ref, ...), custom_call_target="tpu_custom_call" | custom-call | flops 42598400 | bytes 5324800 | tf_op jit(solution)/shard_map/pallas_call | solution.py:180
  32.7 1.6 %collective-permute-start.8 = (f32[14,8,128]{2,1,0:T(8,128)S(1)}, f32[14,8,128]{2,1,0:T(8,128)S(1)}, u32[]{:S(2)}, u32[]{:S(2)}) collective-permute-start(f32[14,8,128]{2,1,0:T(8,128)S(1)} %get-tuple-element.31), channel_id=1, source_target_pairs={{0,16},{16,0},{1,17},{17,1},{2,18},{18,2},{3,19},{19,3},{4,20},{20... | collective-permute-start | bytes 172040 | tf_op jit(solution)/shard_map/ppermute | solution.py:165
  34.3 2.8 %collective-permute-done.8.refs_0_ = f32[14,8,128]{2,1,0:T(8,128)S(1)} collective-permute-done((f32[14,8,128]{2,1,0:T(8,128)S(1)}, f32[14,8,128]{2,1,0:T(8,128)S(1)}, u32[]{:S(2)}, u32[]{:S(2)}) %collective-permute-start.8) | collective-permute-done | bytes 57376 | tf_op jit(solution)/shard_map/ppermute | solution.py:165
  37.0 0.7 %shard_map.56 = (f32[7,8,128]{2,1,0:T(8,128)S(1)}, f32[7,8,128]{2,1,0:T(8,128)S(1)}) custom-call(s32[5]{0:T(128)S(1)} %stack.31.info_ref, f32[26,8,8,128]{3,2,1,0:T(8,128)S(1)} %get-tuple-element.29.post_ref, f32[26,8,8,128]{3,2,1,0:T(8,128)S(1)} %get-tuple-element.30.halo_ref, f32[14,8,128]{2,1,0:T(8,128)S(1)} %collective-permute-done.8.refs_0_), custom_call_target="tpu_custom_call" | custom-call | flops 2129920 | bytes 266240 | tf_op jit(solution)/shard_map/pallas_call | solution.py:180
  37.7 0.1 collective-permute-start.9
  37.8 1.6 %collective-permute-start.10 = (f32[7,8,128]{2,1,0:T(8,128)S(1)}, f32[7,8,128]{2,1,0:T(8,128)S(1)}, u32[]{:S(2)}, u32[]{:S(2)}) collective-permute-start(f32[7,8,128]{2,1,0:T(8,128)S(1)} %get-tuple-element.33), channel_id=1, source_target_pairs={{4,8},{8,4},{12,0},{0,12},{5,9},{9,5},{13,1},{1,13},{6,10},{10,6},... | collective-permute-start | bytes 86024 | tf_op jit(solution)/shard_map/ppermute | solution.py:166
  39.4 0.0 collective-permute-done.9.refs_1_
  39.4 1.7 %collective-permute-done.10.refs_2_ = f32[7,8,128]{2,1,0:T(8,128)S(1)} collective-permute-done((f32[7,8,128]{2,1,0:T(8,128)S(1)}, f32[7,8,128]{2,1,0:T(8,128)S(1)}, u32[]{:S(2)}, u32[]{:S(2)}) %collective-permute-start.10) | collective-permute-done | bytes 28704 | tf_op jit(solution)/shard_map/ppermute | solution.py:166
  41.2 1.8 %shard_map.57 = (f32[19,8,8,128]{3,2,1,0:T(8,128)}, f32[7,8,8,128]{3,2,1,0:T(8,128)}, f32[32,1,128]{2,1,0:T(1,128)S(1)}) custom-call(s32[5]{0:T(128)S(1)} %stack.31.info_ref, f32[26,8,8,128]{3,2,1,0:T(8,128)S(1)} %get-tuple-element.29.post_ref, f32[26,8,8,128]{3,2,1,0:T(8,128)S(1)} %get-tuple-element.30.halo_ref, ...), custom_call_target="tpu_custom_call" | custom-call | flops 42598400 | bytes 5324800 | tf_op jit(solution)/shard_map/pallas_call | solution.py:180
  43.0 11.3 %all_to_all.5 = f32[32,1,128]{2,1,0:T(1,128)S(1)} all-to-all(f32[32,1,128]{2,1,0:T(1,128)S(1)} %get-tuple-element.36), channel_id=1, replica_groups=mesh['gx'=2,'gy'=4,'gz'=4] {'gx','gy','gz'}, dimensions={0} | all-to-all | bytes 32768 | tf_op jit(solution)/shard_map/all_to_all | solution.py:359
  54.3 0.6 %reduce_sum.9 = f32[]{:T(128)} reduce(f32[32,1,128]{2,1,0:T(1,128)S(1)} %all_to_all.5, f32[]{:T(128)} %constant.40.clone.1), dimensions={0,1,2}, to_apply=%region_0.1 | reduce | flops 4095 | bytes 16392 | tf_op jit(solution)/shard_map/reduce_sum | solution.py:362
Async XLA Ops:
  0.7 1.1 %copy-start = (f32[19,8,8,128]{3,2,1,0:T(8,128)S(1)}, f32[19,8,8,128]{3,2,1,0:T(8,128)}, u32[]{:S(2)}) copy-start(f32[19,8,8,128]{3,2,1,0:T(8,128)} %flow_ref.3) | copy-start | bytes 1867780
  1.8 0.9 %copy-start.1 = (f32[7,8,8,128]{3,2,1,0:T(8,128)S(1)}, f32[7,8,8,128]{3,2,1,0:T(8,128)}, u32[]{:S(2)}) copy-start(f32[7,8,8,128]{3,2,1,0:T(8,128)} %heat_ref.3) | copy-start | bytes 688132
  3.6 7.5 %collective-permute-start.1 = (f32[13,8,128]{2,1,0:T(8,128)S(1)}, f32[13,8,128]{2,1,0:T(8,128)S(1)}, u32[]{:S(2)}, u32[]{:S(2)}) collective-permute-start(f32[13,8,128]{2,1,0:T(8,128)S(1)} %shard_map.50), channel_id=1, source_target_pairs={{1,2},{2,1},{5,6},{6,5},{9,10},{10,9},{13,14},{14,13},{17,18},{18,... | collective-permute-start | bytes 159752 | tf_op jit(solution)/shard_map/ppermute | solution.py:166
  4.3 8.1 %collective-permute-start = (f32[13,8,128]{2,1,0:T(8,128)S(1)}, f32[13,8,128]{2,1,0:T(8,128)S(1)}, u32[]{:S(2)}, u32[]{:S(2)}) collective-permute-start(f32[13,8,128]{2,1,0:T(8,128)S(1)} %shard_map.50), channel_id=1, source_target_pairs={{0,1},{1,0},{2,3},{3,2},{4,5},{5,4},{6,7},{7,6},{8,9},{9,8},{10,11... | collective-permute-start | bytes 159752 | tf_op jit(solution)/shard_map/ppermute | solution.py:166
  13.2 4.2 %collective-permute-start.2 = (f32[14,8,128]{2,1,0:T(8,128)S(1)}, f32[14,8,128]{2,1,0:T(8,128)S(1)}, u32[]{:S(2)}, u32[]{:S(2)}) collective-permute-start(f32[14,8,128]{2,1,0:T(8,128)S(1)} %get-tuple-element.21), channel_id=1, source_target_pairs={{0,16},{16,0},{1,17},{17,1},{2,18},{18,2},{3,19},{19,3},{4,20},{20... | collective-permute-start | bytes 172040 | tf_op jit(solution)/shard_map/ppermute | solution.py:165
  18.2 1.7 %collective-permute-start.3 = (f32[7,8,128]{2,1,0:T(8,128)S(1)}, f32[7,8,128]{2,1,0:T(8,128)S(1)}, u32[]{:S(2)}, u32[]{:S(2)}) collective-permute-start(f32[7,8,128]{2,1,0:T(8,128)S(1)} %get-tuple-element.22), channel_id=1, source_target_pairs={{0,4},{4,0},{8,12},{12,8},{1,5},{5,1},{9,13},{13,9},{2,6},{6,2},{1... | collective-permute-start | bytes 86024 | tf_op jit(solution)/shard_map/ppermute | solution.py:166
  18.2 3.4 %collective-permute-start.4 = (f32[7,8,128]{2,1,0:T(8,128)S(1)}, f32[7,8,128]{2,1,0:T(8,128)S(1)}, u32[]{:S(2)}, u32[]{:S(2)}) collective-permute-start(f32[7,8,128]{2,1,0:T(8,128)S(1)} %get-tuple-element.23), channel_id=1, source_target_pairs={{4,8},{8,4},{12,0},{0,12},{5,9},{9,5},{13,1},{1,13},{6,10},{10,6},... | collective-permute-start | bytes 86024 | tf_op jit(solution)/shard_map/ppermute | solution.py:166
  23.0 4.3 %collective-permute-start.5 = (f32[14,8,128]{2,1,0:T(8,128)S(1)}, f32[14,8,128]{2,1,0:T(8,128)S(1)}, u32[]{:S(2)}, u32[]{:S(2)}) collective-permute-start(f32[14,8,128]{2,1,0:T(8,128)S(1)} %get-tuple-element.26), channel_id=1, source_target_pairs={{0,16},{16,0},{1,17},{17,1},{2,18},{18,2},{3,19},{19,3},{4,20},{20... | collective-permute-start | bytes 172040 | tf_op jit(solution)/shard_map/ppermute | solution.py:165
  27.9 1.7 %collective-permute-start.6 = (f32[7,8,128]{2,1,0:T(8,128)S(1)}, f32[7,8,128]{2,1,0:T(8,128)S(1)}, u32[]{:S(2)}, u32[]{:S(2)}) collective-permute-start(f32[7,8,128]{2,1,0:T(8,128)S(1)} %get-tuple-element.27), channel_id=1, source_target_pairs={{0,4},{4,0},{8,12},{12,8},{1,5},{5,1},{9,13},{13,9},{2,6},{6,2},{1... | collective-permute-start | bytes 86024 | tf_op jit(solution)/shard_map/ppermute | solution.py:166
  28.0 3.4 %collective-permute-start.7 = (f32[7,8,128]{2,1,0:T(8,128)S(1)}, f32[7,8,128]{2,1,0:T(8,128)S(1)}, u32[]{:S(2)}, u32[]{:S(2)}) collective-permute-start(f32[7,8,128]{2,1,0:T(8,128)S(1)} %get-tuple-element.28), channel_id=1, source_target_pairs={{4,8},{8,4},{12,0},{0,12},{5,9},{9,5},{13,1},{1,13},{6,10},{10,6},... | collective-permute-start | bytes 86024 | tf_op jit(solution)/shard_map/ppermute | solution.py:166
  32.7 4.3 %collective-permute-start.8 = (f32[14,8,128]{2,1,0:T(8,128)S(1)}, f32[14,8,128]{2,1,0:T(8,128)S(1)}, u32[]{:S(2)}, u32[]{:S(2)}) collective-permute-start(f32[14,8,128]{2,1,0:T(8,128)S(1)} %get-tuple-element.31), channel_id=1, source_target_pairs={{0,16},{16,0},{1,17},{17,1},{2,18},{18,2},{3,19},{19,3},{4,20},{20... | collective-permute-start | bytes 172040 | tf_op jit(solution)/shard_map/ppermute | solution.py:165
  37.7 1.7 %collective-permute-start.9 = (f32[7,8,128]{2,1,0:T(8,128)S(1)}, f32[7,8,128]{2,1,0:T(8,128)S(1)}, u32[]{:S(2)}, u32[]{:S(2)}) collective-permute-start(f32[7,8,128]{2,1,0:T(8,128)S(1)} %get-tuple-element.32), channel_id=1, source_target_pairs={{0,4},{4,0},{8,12},{12,8},{1,5},{5,1},{9,13},{13,9},{2,6},{6,2},{1... | collective-permute-start | bytes 86024 | tf_op jit(solution)/shard_map/ppermute | solution.py:166
  37.8 3.4 %collective-permute-start.10 = (f32[7,8,128]{2,1,0:T(8,128)S(1)}, f32[7,8,128]{2,1,0:T(8,128)S(1)}, u32[]{:S(2)}, u32[]{:S(2)}) collective-permute-start(f32[7,8,128]{2,1,0:T(8,128)S(1)} %get-tuple-element.33), channel_id=1, source_target_pairs={{4,8},{8,4},{12,0},{0,12},{5,9},{9,5},{13,1},{1,13},{6,10},{10,6},... | collective-permute-start | bytes 86024 | tf_op jit(solution)/shard_map/ppermute | solution.py:166

commit v2 on v1

v2 whole, which is shorter than its diff:
```python
import functools

import jax
import jax.numpy as jnp
import numpy as np
from jax import lax
from jax.experimental import pallas as pl
from jax.experimental.pallas import tpu as pltpu
from jax.sharding import PartitionSpec as P

STEPS = 3
TAU_FLOW = 0.6
TAU_HEAT = 0.7
GRAVITY_LIFT = 0.01
HOT_WALL = 0.5
COLD_WALL = -0.5
DIFFUSIVITY = (TAU_HEAT - 0.5) / 4.0

FLOW_SET = [
    (0, 0, 0),
    (1, 0, 0),
    (-1, 0, 0),
    (0, 1, 0),
    (0, -1, 0),
    (0, 0, 1),
    (0, 0, -1),
    (1, 1, 0),
    (-1, -1, 0),
    (1, -1, 0),
    (-1, 1, 0),
    (1, 0, 1),
    (-1, 0, -1),
    (1, 0, -1),
    (-1, 0, 1),
    (0, 1, 1),
    (0, -1, -1),
    (0, 1, -1),
    (0, -1, 1),
]
LATTICE = FLOW_SET + FLOW_SET[:7]
COUNT = len(LATTICE)
NFLOW = len(FLOW_SET)
OPPOSITE = [
    (0 if q < NFLOW else NFLOW) + FLOW_SET.index(tuple(-c for c in LATTICE[q])) for q in range(COUNT)
]
HEAT_WEIGHT = [0.25] + [0.125] * 6
MOVING = {
    (axis, sign): [q for q in range(COUNT) if LATTICE[q][axis] == sign]
    for axis in range(3)
    for sign in (1, -1)
}
FACE = len(MOVING[0, 1])
SLOT = 8


def lanes_of(shape):
    return lax.broadcasted_iota(jnp.int32, shape, 1)


def rows_of(shape):
    return lax.broadcasted_iota(jnp.int32, shape, 0)


def roll(tile, amount, axis):
    size = tile.shape[axis]
    amount = amount % size
    return tile if amount == 0 else pltpu.roll(tile, amount, axis)


def spread(row, shape):
    return jnp.broadcast_to(row, shape)


def total_of(values):
    return functools.reduce(lambda a, b: a + b, values)


def moments(f):
    rho = functools.reduce(lambda a, b: a + b, f[:NFLOW])
    temp = functools.reduce(lambda a, b: a + b, f[NFLOW:])
    diff = {q: f[q] - f[q + 1] for q in range(1, NFLOW, 2)}
    flux = []
    for axis in range(3):
        total = None
        for q in range(1, NFLOW, 2):
            c = LATTICE[q][axis]
            if c:
                assert total is not None or c == 1
                total = diff[q] if total is None else total + diff[q] if c == 1 else total - diff[q]
        flux.append(total)
    push = GRAVITY_LIFT * rho * temp
    inverse = 1.0 / rho
    return rho, temp, push, flux[0] * inverse, flux[1] * inverse, (flux[2] + 0.5 * push) * inverse


def collide(f):
    rho, temp, push, ux, uy, uz = moments(f)
    u = (ux, uy, uz)
    keep = 1.0 - 1.0 / TAU_FLOW
    scale = rho * (1.0 / TAU_FLOW / 36.0)
    source = push * ((1.0 - 0.5 / TAU_FLOW) / 36.0)
    base = scale * (1.0 - 1.5 * (ux * ux + uy * uy + uz * uz)) - 3.0 * source * uz
    linear, square = 3.0 * scale, 4.5 * scale
    push1, push2 = 3.0 * source, 9.0 * source
    out = [None] * COUNT
    out[0] = keep * f[0] + 12.0 * base
    for q in range(1, NFLOW, 2):
        c = LATTICE[q]
        along = None
        for axis in range(3):
            if c[axis]:
                along = u[axis] if along is None else along + u[axis] if c[axis] == 1 else along - u[axis]
        inner = square * along
        odd = linear * along
        if c[2] == 1:
            inner, odd = inner + push2, odd + push1
        elif c[2] == -1:
            inner, odd = inner - push2, odd - push1
        even = base + inner * along
        if q < 7:
            even, odd = 2.0 * even, 2.0 * odd
        out[q] = keep * f[q] + (even + odd)
        out[q + 1] = keep * f[q + 1] + (even - odd)
    keep = 1.0 - 1.0 / TAU_HEAT
    out[NFLOW] = keep * f[NFLOW] + (HEAT_WEIGHT[0] / TAU_HEAT) * temp
    rest = (HEAT_WEIGHT[1] / TAU_HEAT) * temp
    for axis in range(3):
        q = NFLOW + 1 + 2 * axis
        drift = 4.0 * rest * u[axis]
        out[q] = keep * f[q] + (rest + drift)
        out[q + 1] = keep * f[q + 1] + (rest - drift)
    return out


def parity(axis):
    return lax.axis_index(axis) % 2 == 1


def send(outs, up, down, odd):
    if len(outs) == 1:
        for j, tile in enumerate(up + down):
            outs[0][j] = tile
    else:
        for j in range(len(up)):
            outs[0][j] = jnp.where(odd, down[j], up[j])
            outs[1][j] = jnp.where(odd, up[j], down[j])


def received(ins, odd, count):
    if len(ins) == 1:
        return {1: lambda j: ins[0][j], -1: lambda j: ins[0][count + j]}
    return {
        1: lambda j: jnp.where(odd, ins[0][j], ins[1][j]),
        -1: lambda j: jnp.where(odd, ins[1][j], ins[0][j]),
    }


def swap_pairs(size, periodic):
    first = [(i, i + 1) for i in range(0, size - 1, 2)]
    second = [(i, i + 1) for i in range(1, size - 1, 2)] + ([(size - 1, 0)] if periodic else [])
    return [[p for a, b in pairs for p in ((a, b), (b, a))] for pairs in (first, second)]


def swap(buffers, axis, size, periodic=True):
    if size == 1:
        return list(buffers)
    routes = swap_pairs(size, periodic)
    return [lax.ppermute(b, axis, route) for b, route in zip(buffers, routes)]


def swap_corners(buffers, nx, ny):
    routes = [[(0, 0)], []] if ny == 1 else swap_pairs(ny, True)
    moved = {}
    for way in (1, -1):
        if way == -1 and nx <= 2:
            moved[way] = moved[1]
            continue
        moved[way] = [
            lax.ppermute(
                b,
                ("gx", "gy"),
                [(x * ny + i, (x + way) % nx * ny + j) for x in range(nx) for i, j in route],
            )
            for b, route in zip(buffers, routes)
        ]
    return moved


def call(kernel, ins, outs, flops, scratch=(), in_space=pltpu.VMEM, out_space=None, sems=0):
    out_space = [pltpu.VMEM] * len(outs) if out_space is None else out_space
    return pl.pallas_call(
        kernel,
        out_shape=[jax.ShapeDtypeStruct(s, jnp.float32) for s in outs],
        in_specs=[pl.BlockSpec(memory_space=in_space)] * len(ins),
        out_specs=[pl.BlockSpec(memory_space=s) for s in out_space],
        scratch_shapes=[pltpu.VMEM(s, jnp.float32) for s in scratch]
        + ([pltpu.SemaphoreType.DMA((sems,))] if sems else []),
        compiler_params=pltpu.CompilerParams(vmem_limit_bytes=12 * 2**20),
        cost_estimate=pl.CostEstimate(flops=flops, bytes_accessed=flops // 8, transcendentals=0),
    )(*ins)


def per_device(sizes, flow, heat):
    X, Y, Z = flow.shape[1:]
    slots = Z // SLOT
    nx, ny, nz = (sizes[a] for a in ("gx", "gy", "gz"))
    assert all(n == 1 or n % 2 == 0 for n in (nx, ny, nz))
    assert 2 * STEPS <= SLOT and STEPS <= Z and Z % SLOT == 0
    assert slots % X == 0 and FACE <= X and FACE <= slots and Y >= 4
    share = slots // X
    ztiles = -(-COUNT // share)
    tile = (Y, Z)
    bx = 1 if nx <= 2 else 2
    by = 1 if ny <= 2 else 2
    ways = 1 if nx <= 2 else 2
    big, ring = (COUNT, X, Y, Z), (COUNT, Y, Z)
    message_shapes = (
        [(2 * (FACE + 1) // bx, Y, Z)] * bx
        + [(2 * (FACE + 1) // by, X, Z)] * by
        + [(2 // by, Y, Z)] * by
    )
    work = COUNT * X * Y * Z * 10
    start = (X - 1) * SLOT

    def whole(flow_ref, heat_ref):
        return lambda q, x: flow_ref[q, x] if q < NFLOW else heat_ref[q - NFLOW, x]

    def pack_z(flow_ref, heat_ref, pack_ref):
        get = whole(flow_ref, heat_ref)
        lane = lanes_of(tile)
        for t in range(ztiles):
            packed = None
            for k, q in enumerate(range(t * share, min((t + 1) * share, COUNT))):
                for x in range(X):
                    slot = k * X + x
                    moved = roll(get(q, x), STEPS + SLOT * slot, 1)
                    packed = moved if slot == 0 else jnp.where(lane >= SLOT * slot, moved, packed)
            pack_ref[t] = packed

    def first_main(flow_ref, heat_ref, post_ref):
        get = whole(flow_ref, heat_ref)
        for x in range(X):
            for q, value in enumerate(collide([get(q, x) for q in range(COUNT)])):
                post_ref[q, x] = value

    def emit(post_ref, ring_ref, outs):
        x_outs, outs = outs[:bx], outs[bx:]
        y_outs, edge_outs = outs[:by], outs[by:]
        lane, sub, subx = lanes_of(tile), rows_of(tile), rows_of((X, Z))
        sent = []
        for sign, x, at in ((1, X - 1, start), (-1, 0, 0)):
            packed = None
            for j, q in enumerate(MOVING[0, sign]):
                moved = roll(ring_ref[q], SLOT * j - at, 1)
                packed = moved if j == 0 else jnp.where(lane >= SLOT * j, moved, packed)
            sent.append([post_ref[q, x] for q in MOVING[0, sign]] + [packed])
        send(x_outs, sent[0], sent[1], parity("gx"))
        odd = parity("gy")
        rows, edges = [], []
        for sign, y in ((1, Y - 1), (-1, 0)):
            packed = None
            for j, q in enumerate(MOVING[1, sign]):
                row = spread(ring_ref[q, y : y + 1, :], (X, Z))
                packed = row if j == 0 else jnp.where(subx == j, row, packed)
            rows.append([post_ref[q, :, y, :] for q in MOVING[1, sign]] + [packed])
            edge = None
            for k, cx in enumerate((1, -1)):
                q = LATTICE.index((cx, sign, 0))
                x = X - 1 if cx == 1 else 0
                main = spread(post_ref[q, x, y : y + 1, :], tile)
                halo = spread(ring_ref[q, y : y + 1, :], tile)
                edge = main if k == 0 else jnp.where(sub == k, main, edge)
                edge = jnp.where(sub == k + 2, halo, edge)
            edges.append([edge])
        send(y_outs, rows[0], rows[1], odd)
        send(edge_outs, edges[0], edges[1], odd)

    def first_halo(za_ref, zb_ref, post_ref, ring_ref, *outs):
        odd = parity("gz")
        inner = lanes_of(tile) % SLOT < STEPS
        f = []
        for t in range(ztiles):
            a, b = za_ref[t], zb_ref[t]
            merged = jnp.where(inner, jnp.where(odd, a, b), jnp.where(odd, b, a))
            for k, q in enumerate(range(t * share, min((t + 1) * share, COUNT))):
                f.append(roll(merged, -k * X * SLOT, 1))
        for q, value in enumerate(collide(f)):
            ring_ref[q] = value
        emit(post_ref, ring_ref, outs)

    def stream(post_ref, ring_ref, refs, yrow, state, state_ring, done):
        x_refs, refs = refs[:bx], refs[bx:]
        y_refs, refs = refs[:by], refs[by:]
        odd_y = parity("gy")
        from_x = received(x_refs, parity("gx"), FACE + 1)
        from_y = received(y_refs, odd_y, FACE + 1)
        from_edge = {
            (way, sign): received(refs[i * by : (i + 1) * by], odd_y, 1)[sign](0)
            for way, i in ((1, 0), (-1, ways - 1))
            for sign in (1, -1)
        }
        lane, sub = lanes_of(tile), rows_of(tile)
        ends = {1: lane == 0, -1: lane == Z - 1}
        on_wall = {
            1: ends[1] & (lax.axis_index("gz") == 0),
            -1: ends[-1] & (lax.axis_index("gz") == nz - 1),
        }
        borders = {1: sub == 0, -1: sub == Y - 1}
        x_slot = {1: lane < SLOT, -1: lane >= start}
        x_ring = {sign: from_x[sign](FACE) for sign in (1, -1)}
        y_ring = {sign: from_y[sign](FACE) for sign in (1, -1)}
        for sign in (1, -1):
            for j in range(FACE):
                yrow[j if sign == 1 else FACE + j] = from_y[sign](j)

        def ring_of(q):
            cx, cy, _ = LATTICE[q]
            t = ring_ref[q]
            if cx:
                j = MOVING[0, cx].index(q)
                edge = roll(x_ring[cx], (0 if cx == 1 else start) - SLOT * j, 1)
                t = jnp.where(x_slot[cx], edge, roll(t, SLOT * cx, 1))
            if cy:
                j = MOVING[1, cy].index(q)
                row = spread(y_ring[cy][j : j + 1, :], tile)
                if cx:
                    k = 2 if cx == 1 else 3
                    corner = roll(spread(from_edge[cx, cy][k : k + 1, :], tile), -start * cx, 1)
                    row = jnp.where(x_slot[cx], corner, roll(row, SLOT * cx, 1))
                t = jnp.where(borders[cy], row, roll(t, cy, 0))
            return t

        for q in range(COUNT):
            cx, cy, cz = LATTICE[q]
            around = ring_of(q) if cz or state_ring is not None else None
            grown = roll(around, cz, 1) if cz and state_ring is not None else around
            for x in range(X):
                inside = 0 <= x - cx < X
                t = post_ref[q, x - cx] if inside else from_x[cx](MOVING[0, cx].index(q))
                if cy:
                    j = MOVING[1, cy].index(q) + (0 if cy == 1 else FACE)
                    if inside:
                        row = yrow[j, x - cx : x - cx + 1, :]
                    else:
                        k = 0 if cx == 1 else 1
                        row = from_edge[cx, cy][k : k + 1, :]
                    t = jnp.where(borders[cy], spread(row, tile), roll(t, cy, 0))
                if cz:
                    near = SLOT * x + (STEPS - 1 if cz == 1 else STEPS)
                    far = SLOT * x + (STEPS if cz == 1 else STEPS - 1)
                    end = 0 if cz == 1 else Z - 1
                    if state_ring is not None:
                        grown = jnp.where(lane == far, roll(t, far - end + cz, 1), grown)
                    back = post_ref[OPPOSITE[q], x]
                    if q >= NFLOW:
                        wall = HOT_WALL if cz == 1 else COLD_WALL
                        back = 2.0 * HEAT_WEIGHT[q - NFLOW] * wall - back
                    t = jnp.where(ends[cz], roll(around, end - near, 1), roll(t, cz, 1))
                    t = jnp.where(on_wall[cz], back, t)
                state[q, x] = t
            if state_ring is not None:
                state_ring[q] = grown
            done(q)

    def middle(post_ref, ring_ref, *refs):
        given = bx + by * (1 + ways)
        ins, new_ref, new_ring_ref = refs[:given], refs[given], refs[given + 1]
        outs, yrow = refs[given + 2 : -1], refs[-1]
        stream(post_ref, ring_ref, ins, yrow, new_ref, new_ring_ref, lambda q: None)
        for x in range(X):
            for q, value in enumerate(collide([new_ref[q, x] for q in range(COUNT)])):
                new_ref[q, x] = value
        for q, value in enumerate(collide([new_ring_ref[q] for q in range(COUNT)])):
            new_ring_ref[q] = value
        emit(new_ref, new_ring_ref, outs)

    devices = nx * ny * nz

    def final(post_ref, ring_ref, *refs):
        given = bx + by * (1 + ways)
        ins, (flow_ref, heat_ref, part_ref, yrow, state, sems) = refs[:given], refs[given:]
        copies = [
            pltpu.make_async_copy(
                state.at[q], flow_ref.at[q] if q < NFLOW else heat_ref.at[q - NFLOW], sems.at[q]
            )
            for q in range(COUNT)
        ]
        stream(post_ref, ring_ref, ins, yrow, state, None, lambda q: copies[q].start())
        parts = []
        for x in range(X):
            _, temp, _, _, _, uz = moments([state[q, x] for q in range(COUNT)])
            parts.append(uz * temp)
        part = jnp.sum(total_of(parts), axis=0, keepdims=True)
        part_ref[...] = jnp.broadcast_to(part[None], part_ref.shape)
        for copy in copies:
            copy.wait()

    cells = X * Y * Z * devices
    factor = Z * nz / (DIFFUSIVITY * (HOT_WALL - COLD_WALL)) / cells

    def finish(parts_ref, out_ref):
        part = jnp.sum(parts_ref[...], axis=0)
        out_ref[...] = 1.0 + factor * jnp.sum(part, axis=1, keepdims=True)

    def exchange(messages):
        xs, messages = messages[:bx], messages[bx:]
        ys, edges = messages[:by], messages[by:]
        xs = swap(xs, "gx", nx)
        ys = swap(ys, "gy", ny)
        moved = swap_corners(edges, nx, ny)
        edges = moved[1] + (moved[-1] if ways == 2 else [])
        return [*xs, *ys, *edges]

    (zpack,) = call(pack_z, (flow, heat), [(ztiles, Y, Z)], work)
    za, zb = swap([zpack, zpack], "gz", nz, False)
    (post,) = call(first_main, (flow, heat), [big], 20 * work)
    around, *messages = call(first_halo, (za, zb, post), [ring] + message_shapes, 2 * work)
    scratch = [(2 * FACE, X, Z)]
    for step in range(STEPS - 1):
        ins = (post, around, *exchange(messages))
        post, around, *messages = call(middle, ins, [big, ring] + message_shapes, 20 * work, scratch)
    flow, heat, parts = call(
        final,
        (post, around, *exchange(messages)),
        [flow.shape, heat.shape, (devices, 1, Z)],
        20 * work,
        scratch + [big],
        out_space=[pltpu.HBM, pltpu.HBM, pltpu.VMEM],
        sems=COUNT,
    )
    parts = lax.all_to_all(parts, ("gx", "gy", "gz"), 0, 0, tiled=True)
    (nusselt,) = call(finish, (parts,), [(1, 1)], work)
    return flow, heat, nusselt.reshape(())


def solution(mesh):
    placed = P(None, "gx", "gy", "gz")
    return jax.shard_map(
        functools.partial(per_device, dict(mesh.shape)),
        mesh=mesh,
        in_specs=(placed, placed),
        out_specs=(placed, placed, P()),
        check_vma=False,
    )
```

time: 56.9 us -> 47.5 us (0.83)
  waiting for transfers between devices: 14.7 us -> 8.19 us
  starting transfers between devices: 16.4 us -> 21.2 us
  Pallas kernels: 9.04 us -> 4.72 us
  between operations: 2.55 us -> 0.72 us
  blocking collectives: 11.3 us -> 10.4 us
  other arithmetic: 0.63 us -> 0 us
    ppermute x11 -> x17, waiting for transfers between devices: 14.7 us -> 8.19 us  [the longest x6 6.37 us: swap_corners(): lax.ppermute(b, ('gx', 'gy'), [(x * ny + i, (x + way) % nx * ny + j) for...]
    ppermute x11 -> x17, starting transfers between devices: 16.4 us -> 21.2 us  [the longest x11 15.1 us: swap(): return [lax.ppermute(b, axis, route) for b, route in zip(buffers, routes)]]
    pallas_call x9 -> x7, Pallas kernels: 9.04 us -> 4.72 us  [call(): pl.pallas_call(kernel, out_shape=[jax.ShapeDtypeStruct(s, jnp.float32) fo...]
    all_to_all x1, blocking collectives: 11.3 us -> 10.4 us  [per_device(): parts = lax.all_to_all(parts, ('gx', 'gy', 'gz'), 0, 0, tiled=True)]
    reduce_sum x1 -> x0, other arithmetic: 0.63 us -> none  [per_device(): nusselt = 1.0 + factor * jnp.sum(parts)]
  transfers between devices with their start and end apart: 11 -> 17, of which waited for: 7 -> 7; matrix products, arithmetic and copies ran while one was open for 0% -> 0% of each run, Pallas kernels for 2% -> 1%
where the time goes in v2:
time: 47.5 us; the launch traced here: 47.3 us
  starting transfers between devices  21.2 us (45%)
  blocking collectives  10.4 us (22%)
  waiting for transfers between devices  8.19 us (17%)
  Pallas kernels  4.72 us (10%)
  local copies, waits for them, and re-layouts  2.01 us (4%)
  between operations  0.72 us (2%)
    ppermute x11, starting transfers between devices, swap(): return [lax.ppermute(b, axis, route) for b, route in zip(buffers, routes)]  15.1 us
    all_to_all x1, blocking collectives, per_device(): parts = lax.all_to_all(parts, ('gx', 'gy', 'gz'), 0, 0, tiled=True)  10.4 us
    ppermute x6, waiting for transfers between devices, swap_corners(): lax.ppermute(b, ('gx', 'gy'), [(x * ny + i, (x + way) % nx * ny + j) for...  6.37 us
    ppermute x6, starting transfers between devices, swap_corners(): lax.ppermute(b, ('gx', 'gy'), [(x * ny + i, (x + way) % nx * ny + j) for...  6.08 us
    pallas_call x7, Pallas kernels, call(): pl.pallas_call(kernel, out_shape=[jax.ShapeDtypeStruct(s, jnp.float32) fo...  4.72 us
    unnamed x4, local copies, waits for them, and re-layouts  2.01 us
    ppermute x11, waiting for transfers between devices, swap(): return [lax.ppermute(b, axis, route) for b, route in zip(buffers, routes)]  1.83 us
  transfers between devices with their start and end apart: 17, of which 7 were waited for; matrix products, arithmetic and copies ran while one was open for 0% of the time, Pallas kernels for 1%

profile of v2, /device:TPU:0, one launch (start us, length us, event | category | flops | bytes accessed | tf_op | source)
XLA Modules:
  0.0 47.3 jit_solution(10668880055652421823)
XLA Ops:
  0.6 0.0 copy-start
  0.6 1.1 %copy-done = f32[19,8,8,128]{3,2,1,0:T(8,128)S(1)} copy-done((f32[19,8,8,128]{3,2,1,0:T(8,128)S(1)}, f32[19,8,8,128]{3,2,1,0:T(8,128)}, u32[]{:S(2)}) %copy-start) | copy-done | bytes 622616
  1.7 0.0 copy-start.1
  1.7 0.9 %copy-done.1 = f32[7,8,8,128]{3,2,1,0:T(8,128)S(1)} copy-done((f32[7,8,8,128]{3,2,1,0:T(8,128)S(1)}, f32[7,8,8,128]{3,2,1,0:T(8,128)}, u32[]{:S(2)}) %copy-start.1) | copy-done | bytes 229400
  2.6 0.3 shard_map.50
  2.9 0.7 %collective-permute-start.1 = (f32[13,8,128]{2,1,0:T(8,128)S(1)}, f32[13,8,128]{2,1,0:T(8,128)S(1)}, u32[]{:S(2)}, u32[]{:S(2)}) collective-permute-start(f32[13,8,128]{2,1,0:T(8,128)S(1)} %shard_map.50), channel_id=1, source_target_pairs={{1,2},{2,1},{5,6},{6,5},{9,10},{10,9},{13,14},{14,13},{17,18},{18,... | collective-permute-start | bytes 159752 | tf_op jit(solution)/shard_map/ppermute | solution.py:168
  3.6 5.9 %collective-permute-start = (f32[13,8,128]{2,1,0:T(8,128)S(1)}, f32[13,8,128]{2,1,0:T(8,128)S(1)}, u32[]{:S(2)}, u32[]{:S(2)}) collective-permute-start(f32[13,8,128]{2,1,0:T(8,128)S(1)} %shard_map.50), channel_id=1, source_target_pairs={{0,1},{1,0},{2,3},{3,2},{4,5},{5,4},{6,7},{7,6},{8,9},{9,8},{10,11... | collective-permute-start | bytes 159752 | tf_op jit(solution)/shard_map/ppermute | solution.py:168
  9.5 0.3 shard_map.49.post_ref
  9.8 0.0 collective-permute-done.1.zb_ref
  9.9 1.8 %collective-permute-done.za_ref = f32[13,8,128]{2,1,0:T(8,128)S(1)} collective-permute-done((f32[13,8,128]{2,1,0:T(8,128)S(1)}, f32[13,8,128]{2,1,0:T(8,128)S(1)}, u32[]{:S(2)}, u32[]{:S(2)}) %collective-permute-start) | collective-permute-done | bytes 53280 | tf_op jit(solution)/shard_map/ppermute | solution.py:168
  11.7 0.2 shard_map.51
  11.9 1.5 %collective-permute-start.2 = (f32[14,8,128]{2,1,0:T(8,128)S(1)}, f32[14,8,128]{2,1,0:T(8,128)S(1)}, u32[]{:S(2)}, u32[]{:S(2)}) collective-permute-start(f32[14,8,128]{2,1,0:T(8,128)S(1)} %get-tuple-element.27), channel_id=1, source_target_pairs={{0,16},{16,0},{1,17},{17,1},{2,18},{18,2},{3,19},{19,3},{4,20},{20... | collective-permute-start | bytes 172040 | tf_op jit(solution)/shard_map/ppermute | solution.py:168
  13.4 0.0 collective-permute-start.3
  13.4 1.6 %collective-permute-start.4 = (f32[7,8,128]{2,1,0:T(8,128)S(1)}, f32[7,8,128]{2,1,0:T(8,128)S(1)}, u32[]{:S(2)}, u32[]{:S(2)}) collective-permute-start(f32[7,8,128]{2,1,0:T(8,128)S(1)} %get-tuple-element.29), channel_id=1, source_target_pairs={{4,8},{8,4},{12,0},{0,12},{5,9},{9,5},{13,1},{1,13},{6,10},{10,6},... | collective-permute-start | bytes 86024 | tf_op jit(solution)/shard_map/ppermute | solution.py:168
  15.0 0.1 collective-permute-start.5
  15.2 1.5 %collective-permute-start.6 = (f32[1,8,128]{2,1,0:T(8,128)S(1)}, f32[1,8,128]{2,1,0:T(8,128)S(1)}, u32[]{:S(2)}, u32[]{:S(2)}) collective-permute-start(f32[1,8,128]{2,1,0:T(8,128)S(1)} %get-tuple-element.31), channel_id=1, source_target_pairs={{4,24},{8,20},{12,16},{0,28},{20,8},{24,4},{28,0},{16,12},{5,25},{... | collective-permute-start | bytes 12296 | tf_op jit(solution)/shard_map/ppermute | solution.py:179
  16.7 1.3 %collective-permute-done.5.refs_3_ = f32[1,8,128]{2,1,0:T(8,128)S(1)} collective-permute-done((f32[1,8,128]{2,1,0:T(8,128)S(1)}, f32[1,8,128]{2,1,0:T(8,128)S(1)}, u32[]{:S(2)}, u32[]{:S(2)}) %collective-permute-start.5) | collective-permute-done | bytes 4128 | tf_op jit(solution)/shard_map/ppermute | solution.py:179
  18.1 1.0 %collective-permute-done.6.refs_4_ = f32[1,8,128]{2,1,0:T(8,128)S(1)} collective-permute-done((f32[1,8,128]{2,1,0:T(8,128)S(1)}, f32[1,8,128]{2,1,0:T(8,128)S(1)}, u32[]{:S(2)}, u32[]{:S(2)}) %collective-permute-start.6) | collective-permute-done | bytes 4128 | tf_op jit(solution)/shard_map/ppermute | solution.py:179
  19.1 0.0 collective-permute-done.3.refs_1_
  19.1 0.0 collective-permute-done.4.refs_2_
  19.1 0.0 collective-permute-done.2.refs_0_
  19.1 1.0 %shard_map.52 = (f32[26,8,8,128]{3,2,1,0:T(8,128)S(1)}, f32[26,8,128]{2,1,0:T(8,128)S(1)}, f32[14,8,128]{2,1,0:T(8,128)S(1)}, f32[7,8,128]{2,1,0:T(8,128)S(1)}, ...) custom-call(f32[26,8,8,128]{3,2,1,0:T(8,128)S(1)} %shard_map.49.post_ref, ...), custom_call_target="tpu_custom_call" | custom-call | flops 42598400 | bytes 5324800 | tf_op jit(solution)/shard_map/pallas_call | solution.py:191
  20.1 1.6 %collective-permute-start.7 = (f32[14,8,128]{2,1,0:T(8,128)S(1)}, f32[14,8,128]{2,1,0:T(8,128)S(1)}, u32[]{:S(2)}, u32[]{:S(2)}) collective-permute-start(f32[14,8,128]{2,1,0:T(8,128)S(1)} %get-tuple-element.34), channel_id=1, source_target_pairs={{0,16},{16,0},{1,17},{17,1},{2,18},{18,2},{3,19},{19,3},{4,20},{20... | collective-permute-start | bytes 172040 | tf_op jit(solution)/shard_map/ppermute | solution.py:168
  21.6 0.2 collective-permute-start.8
  21.9 0.4 collective-permute-start.9
  22.3 0.4 collective-permute-start.10
  22.6 2.3 %collective-permute-start.11 = (f32[1,8,128]{2,1,0:T(8,128)S(1)}, f32[1,8,128]{2,1,0:T(8,128)S(1)}, u32[]{:S(2)}, u32[]{:S(2)}) collective-permute-start(f32[1,8,128]{2,1,0:T(8,128)S(1)} %get-tuple-element.38), channel_id=1, source_target_pairs={{4,24},{8,20},{12,16},{0,28},{20,8},{24,4},{28,0},{16,12},{5,25},{... | collective-permute-start | bytes 12296 | tf_op jit(solution)/shard_map/ppermute | solution.py:179
  25.0 0.3 collective-permute-done.10.refs_3_
  25.3 1.3 %collective-permute-done.11.refs_4_ = f32[1,8,128]{2,1,0:T(8,128)S(1)} collective-permute-done((f32[1,8,128]{2,1,0:T(8,128)S(1)}, f32[1,8,128]{2,1,0:T(8,128)S(1)}, u32[]{:S(2)}, u32[]{:S(2)}) %collective-permute-start.11) | collective-permute-done | bytes 4128 | tf_op jit(solution)/shard_map/ppermute | solution.py:179
  26.6 0.0 collective-permute-done.8.refs_1_
  26.6 0.0 collective-permute-done.9.refs_2_
  26.6 0.0 collective-permute-done.7.refs_0_
  26.6 1.0 %shard_map.53 = (f32[26,8,8,128]{3,2,1,0:T(8,128)S(1)}, f32[26,8,128]{2,1,0:T(8,128)S(1)}, f32[14,8,128]{2,1,0:T(8,128)S(1)}, f32[7,8,128]{2,1,0:T(8,128)S(1)}, ...) custom-call(f32[26,8,8,128]{3,2,1,0:T(8,128)S(1)} %get-tuple-element.32.post_ref, ...), custom_call_target="tpu_custom_call" | custom-call | flops 42598400 | bytes 5324800 | tf_op jit(solution)/shard_map/pallas_call | solution.py:191
  27.6 1.6 %collective-permute-start.12 = (f32[14,8,128]{2,1,0:T(8,128)S(1)}, f32[14,8,128]{2,1,0:T(8,128)S(1)}, u32[]{:S(2)}, u32[]{:S(2)}) collective-permute-start(f32[14,8,128]{2,1,0:T(8,128)S(1)} %get-tuple-element.41), channel_id=1, source_target_pairs={{0,16},{16,0},{1,17},{17,1},{2,18},{18,2},{3,19},{19,3},{4,20},{20... | collective-permute-start | bytes 172040 | tf_op jit(solution)/shard_map/ppermute | solution.py:168
  29.1 0.0 collective-permute-start.13
  29.1 1.6 %collective-permute-start.14 = (f32[7,8,128]{2,1,0:T(8,128)S(1)}, f32[7,8,128]{2,1,0:T(8,128)S(1)}, u32[]{:S(2)}, u32[]{:S(2)}) collective-permute-start(f32[7,8,128]{2,1,0:T(8,128)S(1)} %get-tuple-element.43), channel_id=1, source_target_pairs={{4,8},{8,4},{12,0},{0,12},{5,9},{9,5},{13,1},{1,13},{6,10},{10,6},... | collective-permute-start | bytes 86024 | tf_op jit(solution)/shard_map/ppermute | solution.py:168
  30.7 0.1 collective-permute-start.15
  30.9 1.5 %collective-permute-start.16 = (f32[1,8,128]{2,1,0:T(8,128)S(1)}, f32[1,8,128]{2,1,0:T(8,128)S(1)}, u32[]{:S(2)}, u32[]{:S(2)}) collective-permute-start(f32[1,8,128]{2,1,0:T(8,128)S(1)} %get-tuple-element.45), channel_id=1, source_target_pairs={{4,24},{8,20},{12,16},{0,28},{20,8},{24,4},{28,0},{16,12},{5,25},{... | collective-permute-start | bytes 12296 | tf_op jit(solution)/shard_map/ppermute | solution.py:179
  32.4 1.3 %collective-permute-done.15.refs_3_ = f32[1,8,128]{2,1,0:T(8,128)S(1)} collective-permute-done((f32[1,8,128]{2,1,0:T(8,128)S(1)}, f32[1,8,128]{2,1,0:T(8,128)S(1)}, u32[]{:S(2)}, u32[]{:S(2)}) %collective-permute-start.15) | collective-permute-done | bytes 4128 | tf_op jit(solution)/shard_map/ppermute | solution.py:179
  33.8 1.0 %collective-permute-done.16.refs_4_ = f32[1,8,128]{2,1,0:T(8,128)S(1)} collective-permute-done((f32[1,8,128]{2,1,0:T(8,128)S(1)}, f32[1,8,128]{2,1,0:T(8,128)S(1)}, u32[]{:S(2)}, u32[]{:S(2)}) %collective-permute-start.16) | collective-permute-done | bytes 4128 | tf_op jit(solution)/shard_map/ppermute | solution.py:179
  34.8 0.0 collective-permute-done.13.refs_1_
  34.8 0.0 collective-permute-done.14.refs_2_
  34.8 0.0 collective-permute-done.12.refs_0_
  34.8 1.4 %shard_map.54 = (f32[19,8,8,128]{3,2,1,0:T(8,128)}, f32[7,8,8,128]{3,2,1,0:T(8,128)}, f32[32,1,128]{2,1,0:T(1,128)S(1)}) custom-call(f32[26,8,8,128]{3,2,1,0:T(8,128)S(1)} %get-tuple-element.39.post_ref, f32[26,8,128]{2,1,0:T(8,128)S(1)} %get-tuple-element.40.ring_ref, f32[14,8,128]{2,1,0:T(8,128)S(1)} %collective-permute-done.12.refs_0_, ...), custom_call_target="tpu_custom_call" | custom-call | flops 42598400 | bytes 5324800 | tf_op jit(solution)/shard_map/pallas_call | solution.py:191
  36.2 10.4 %all_to_all.5.parts_ref = f32[32,1,128]{2,1,0:T(1,128)S(1)} all-to-all(f32[32,1,128]{2,1,0:T(1,128)S(1)} %get-tuple-element.48), channel_id=1, replica_groups=mesh['gx'=2,'gy'=4,'gz'=4] {'gx','gy','gz'}, dimensions={0} | all-to-all | bytes 32768 | tf_op jit(solution)/shard_map/all_to_all | solution.py:431
  46.7 0.6 %shard_map.55 = f32[1,1]{1,0:T(1,128)} custom-call(f32[32,1,128]{2,1,0:T(1,128)S(1)} %all_to_all.5.parts_ref), custom_call_target="tpu_custom_call" | custom-call | flops 2129920 | bytes 266240 | tf_op jit(solution)/shard_map/pallas_call | solution.py:191
Async XLA Ops:
  0.6 1.1 %copy-start = (f32[19,8,8,128]{3,2,1,0:T(8,128)S(1)}, f32[19,8,8,128]{3,2,1,0:T(8,128)}, u32[]{:S(2)}) copy-start(f32[19,8,8,128]{3,2,1,0:T(8,128)} %flow_ref.3) | copy-start | bytes 1867780
  1.7 0.9 %copy-start.1 = (f32[7,8,8,128]{3,2,1,0:T(8,128)S(1)}, f32[7,8,8,128]{3,2,1,0:T(8,128)}, u32[]{:S(2)}) copy-start(f32[7,8,8,128]{3,2,1,0:T(8,128)} %heat_ref.3) | copy-start | bytes 688132
  2.9 6.9 %collective-permute-start.1 = (f32[13,8,128]{2,1,0:T(8,128)S(1)}, f32[13,8,128]{2,1,0:T(8,128)S(1)}, u32[]{:S(2)}, u32[]{:S(2)}) collective-permute-start(f32[13,8,128]{2,1,0:T(8,128)S(1)} %shard_map.50), channel_id=1, source_target_pairs={{1,2},{2,1},{5,6},{6,5},{9,10},{10,9},{13,14},{14,13},{17,18},{18,... | collective-permute-start | bytes 159752 | tf_op jit(solution)/shard_map/ppermute | solution.py:168
  3.6 8.1 %collective-permute-start = (f32[13,8,128]{2,1,0:T(8,128)S(1)}, f32[13,8,128]{2,1,0:T(8,128)S(1)}, u32[]{:S(2)}, u32[]{:S(2)}) collective-permute-start(f32[13,8,128]{2,1,0:T(8,128)S(1)} %shard_map.50), channel_id=1, source_target_pairs={{0,1},{1,0},{2,3},{3,2},{4,5},{5,4},{6,7},{7,6},{8,9},{9,8},{10,11... | collective-permute-start | bytes 159752 | tf_op jit(solution)/shard_map/ppermute | solution.py:168
  11.9 7.2 %collective-permute-start.2 = (f32[14,8,128]{2,1,0:T(8,128)S(1)}, f32[14,8,128]{2,1,0:T(8,128)S(1)}, u32[]{:S(2)}, u32[]{:S(2)}) collective-permute-start(f32[14,8,128]{2,1,0:T(8,128)S(1)} %get-tuple-element.27), channel_id=1, source_target_pairs={{0,16},{16,0},{1,17},{17,1},{2,18},{18,2},{3,19},{19,3},{4,20},{20... | collective-permute-start | bytes 172040 | tf_op jit(solution)/shard_map/ppermute | solution.py:168
  13.4 5.7 %collective-permute-start.3 = (f32[7,8,128]{2,1,0:T(8,128)S(1)}, f32[7,8,128]{2,1,0:T(8,128)S(1)}, u32[]{:S(2)}, u32[]{:S(2)}) collective-permute-start(f32[7,8,128]{2,1,0:T(8,128)S(1)} %get-tuple-element.28), channel_id=1, source_target_pairs={{0,4},{4,0},{8,12},{12,8},{1,5},{5,1},{9,13},{13,9},{2,6},{6,2},{1... | collective-permute-start | bytes 86024 | tf_op jit(solution)/shard_map/ppermute | solution.py:168
  13.4 5.7 %collective-permute-start.4 = (f32[7,8,128]{2,1,0:T(8,128)S(1)}, f32[7,8,128]{2,1,0:T(8,128)S(1)}, u32[]{:S(2)}, u32[]{:S(2)}) collective-permute-start(f32[7,8,128]{2,1,0:T(8,128)S(1)} %get-tuple-element.29), channel_id=1, source_target_pairs={{4,8},{8,4},{12,0},{0,12},{5,9},{9,5},{13,1},{1,13},{6,10},{10,6},... | collective-permute-start | bytes 86024 | tf_op jit(solution)/shard_map/ppermute | solution.py:168
  15.0 3.0 %collective-permute-start.5 = (f32[1,8,128]{2,1,0:T(8,128)S(1)}, f32[1,8,128]{2,1,0:T(8,128)S(1)}, u32[]{:S(2)}, u32[]{:S(2)}) collective-permute-start(f32[1,8,128]{2,1,0:T(8,128)S(1)} %get-tuple-element.30), channel_id=1, source_target_pairs={{0,20},{4,16},{8,28},{12,24},{16,4},{20,0},{24,12},{28,8},{1,21},{... | collective-permute-start | bytes 12296 | tf_op jit(solution)/shard_map/ppermute | solution.py:179
  15.2 3.9 %collective-permute-start.6 = (f32[1,8,128]{2,1,0:T(8,128)S(1)}, f32[1,8,128]{2,1,0:T(8,128)S(1)}, u32[]{:S(2)}, u32[]{:S(2)}) collective-permute-start(f32[1,8,128]{2,1,0:T(8,128)S(1)} %get-tuple-element.31), channel_id=1, source_target_pairs={{4,24},{8,20},{12,16},{0,28},{20,8},{24,4},{28,0},{16,12},{5,25},{... | collective-permute-start | bytes 12296 | tf_op jit(solution)/shard_map/ppermute | solution.py:179
  20.1 6.5 %collective-permute-start.7 = (f32[14,8,128]{2,1,0:T(8,128)S(1)}, f32[14,8,128]{2,1,0:T(8,128)S(1)}, u32[]{:S(2)}, u32[]{:S(2)}) collective-permute-start(f32[14,8,128]{2,1,0:T(8,128)S(1)} %get-tuple-element.34), channel_id=1, source_target_pairs={{0,16},{16,0},{1,17},{17,1},{2,18},{18,2},{3,19},{19,3},{4,20},{20... | collective-permute-start | bytes 172040 | tf_op jit(solution)/shard_map/ppermute | solution.py:168
  21.6 4.9 %collective-permute-start.8 = (f32[7,8,128]{2,1,0:T(8,128)S(1)}, f32[7,8,128]{2,1,0:T(8,128)S(1)}, u32[]{:S(2)}, u32[]{:S(2)}) collective-permute-start(f32[7,8,128]{2,1,0:T(8,128)S(1)} %get-tuple-element.35), channel_id=1, source_target_pairs={{0,4},{4,0},{8,12},{12,8},{1,5},{5,1},{9,13},{13,9},{2,6},{6,2},{1... | collective-permute-start | bytes 86024 | tf_op jit(solution)/shard_map/ppermute | solution.py:168
  21.9 4.7 %collective-permute-start.9 = (f32[7,8,128]{2,1,0:T(8,128)S(1)}, f32[7,8,128]{2,1,0:T(8,128)S(1)}, u32[]{:S(2)}, u32[]{:S(2)}) collective-permute-start(f32[7,8,128]{2,1,0:T(8,128)S(1)} %get-tuple-element.36), channel_id=1, source_target_pairs={{4,8},{8,4},{12,0},{0,12},{5,9},{9,5},{13,1},{1,13},{6,10},{10,6},... | collective-permute-start | bytes 86024 | tf_op jit(solution)/shard_map/ppermute | solution.py:168
  22.3 3.0 %collective-permute-start.10 = (f32[1,8,128]{2,1,0:T(8,128)S(1)}, f32[1,8,128]{2,1,0:T(8,128)S(1)}, u32[]{:S(2)}, u32[]{:S(2)}) collective-permute-start(f32[1,8,128]{2,1,0:T(8,128)S(1)} %get-tuple-element.37), channel_id=1, source_target_pairs={{0,20},{4,16},{8,28},{12,24},{16,4},{20,0},{24,12},{28,8},{1,21},{... | collective-permute-start | bytes 12296 | tf_op jit(solution)/shard_map/ppermute | solution.py:179
  22.6 3.9 %collective-permute-start.11 = (f32[1,8,128]{2,1,0:T(8,128)S(1)}, f32[1,8,128]{2,1,0:T(8,128)S(1)}, u32[]{:S(2)}, u32[]{:S(2)}) collective-permute-start(f32[1,8,128]{2,1,0:T(8,128)S(1)} %get-tuple-element.38), channel_id=1, source_target_pairs={{4,24},{8,20},{12,16},{0,28},{20,8},{24,4},{28,0},{16,12},{5,25},{... | collective-permute-start | bytes 12296 | tf_op jit(solution)/shard_map/ppermute | solution.py:179
  27.6 7.3 %collective-permute-start.12 = (f32[14,8,128]{2,1,0:T(8,128)S(1)}, f32[14,8,128]{2,1,0:T(8,128)S(1)}, u32[]{:S(2)}, u32[]{:S(2)}) collective-permute-start(f32[14,8,128]{2,1,0:T(8,128)S(1)} %get-tuple-element.41), channel_id=1, source_target_pairs={{0,16},{16,0},{1,17},{17,1},{2,18},{18,2},{3,19},{19,3},{4,20},{20... | collective-permute-start | bytes 172040 | tf_op jit(solution)/shard_map/ppermute | solution.py:168
  29.1 5.7 %collective-permute-start.13 = (f32[7,8,128]{2,1,0:T(8,128)S(1)}, f32[7,8,128]{2,1,0:T(8,128)S(1)}, u32[]{:S(2)}, u32[]{:S(2)}) collective-permute-start(f32[7,8,128]{2,1,0:T(8,128)S(1)} %get-tuple-element.42), channel_id=1, source_target_pairs={{0,4},{4,0},{8,12},{12,8},{1,5},{5,1},{9,13},{13,9},{2,6},{6,2},{1... | collective-permute-start | bytes 86024 | tf_op jit(solution)/shard_map/ppermute | solution.py:168
  29.1 5.7 %collective-permute-start.14 = (f32[7,8,128]{2,1,0:T(8,128)S(1)}, f32[7,8,128]{2,1,0:T(8,128)S(1)}, u32[]{:S(2)}, u32[]{:S(2)}) collective-permute-start(f32[7,8,128]{2,1,0:T(8,128)S(1)} %get-tuple-element.43), channel_id=1, source_target_pairs={{4,8},{8,4},{12,0},{0,12},{5,9},{9,5},{13,1},{1,13},{6,10},{10,6},... | collective-permute-start | bytes 86024 | tf_op jit(solution)/shard_map/ppermute | solution.py:168
  30.7 3.0 %collective-permute-start.15 = (f32[1,8,128]{2,1,0:T(8,128)S(1)}, f32[1,8,128]{2,1,0:T(8,128)S(1)}, u32[]{:S(2)}, u32[]{:S(2)}) collective-permute-start(f32[1,8,128]{2,1,0:T(8,128)S(1)} %get-tuple-element.44), channel_id=1, source_target_pairs={{0,20},{4,16},{8,28},{12,24},{16,4},{20,0},{24,12},{28,8},{1,21},{... | collective-permute-start | bytes 12296 | tf_op jit(solution)/shard_map/ppermute | solution.py:179
  30.9 3.9 %collective-permute-start.16 = (f32[1,8,128]{2,1,0:T(8,128)S(1)}, f32[1,8,128]{2,1,0:T(8,128)S(1)}, u32[]{:S(2)}, u32[]{:S(2)}) collective-permute-start(f32[1,8,128]{2,1,0:T(8,128)S(1)} %get-tuple-element.45), channel_id=1, source_target_pairs={{4,24},{8,20},{12,16},{0,28},{20,8},{24,4},{28,0},{16,12},{5,25},{... | collective-permute-start | bytes 12296 | tf_op jit(solution)/shard_map/ppermute | solution.py:179

commit v3 on v2

v3 whole, which is shorter than its diff:
```python
import functools

import jax
import jax.numpy as jnp
import numpy as np
from jax import lax
from jax.experimental import pallas as pl
from jax.experimental.pallas import tpu as pltpu
from jax.sharding import PartitionSpec as P

STEPS = 3
TAU_FLOW = 0.6
TAU_HEAT = 0.7
GRAVITY_LIFT = 0.01
HOT_WALL = 0.5
COLD_WALL = -0.5
DIFFUSIVITY = (TAU_HEAT - 0.5) / 4.0

FLOW_SET = [
    (0, 0, 0),
    (1, 0, 0),
    (-1, 0, 0),
    (0, 1, 0),
    (0, -1, 0),
    (0, 0, 1),
    (0, 0, -1),
    (1, 1, 0),
    (-1, -1, 0),
    (1, -1, 0),
    (-1, 1, 0),
    (1, 0, 1),
    (-1, 0, -1),
    (1, 0, -1),
    (-1, 0, 1),
    (0, 1, 1),
    (0, -1, -1),
    (0, 1, -1),
    (0, -1, 1),
]
LATTICE = FLOW_SET + FLOW_SET[:7]
COUNT = len(LATTICE)
NFLOW = len(FLOW_SET)
OPPOSITE = [
    (0 if q < NFLOW else NFLOW) + FLOW_SET.index(tuple(-c for c in LATTICE[q])) for q in range(COUNT)
]
HEAT_WEIGHT = [0.25] + [0.125] * 6
MOVING = {
    (axis, sign): [q for q in range(COUNT) if LATTICE[q][axis] == sign]
    for axis in range(3)
    for sign in (1, -1)
}
FACE = len(MOVING[0, 1])
SLOT = 8


def lanes_of(shape):
    return lax.broadcasted_iota(jnp.int32, shape, 1)


def rows_of(shape):
    return lax.broadcasted_iota(jnp.int32, shape, 0)


def roll(tile, amount, axis):
    size = tile.shape[axis]
    amount = amount % size
    return tile if amount == 0 else pltpu.roll(tile, amount, axis)


def spread(row, shape):
    return jnp.broadcast_to(row, shape)


def total_of(values):
    return functools.reduce(lambda a, b: a + b, values)


def moments(f):
    rho = functools.reduce(lambda a, b: a + b, f[:NFLOW])
    temp = functools.reduce(lambda a, b: a + b, f[NFLOW:])
    diff = {q: f[q] - f[q + 1] for q in range(1, NFLOW, 2)}
    flux = []
    for axis in range(3):
        total = None
        for q in range(1, NFLOW, 2):
            c = LATTICE[q][axis]
            if c:
                assert total is not None or c == 1
                total = diff[q] if total is None else total + diff[q] if c == 1 else total - diff[q]
        flux.append(total)
    push = GRAVITY_LIFT * rho * temp
    inverse = 1.0 / rho
    return rho, temp, push, flux[0] * inverse, flux[1] * inverse, (flux[2] + 0.5 * push) * inverse


def collide(f):
    rho, temp, push, ux, uy, uz = moments(f)
    u = (ux, uy, uz)
    keep = 1.0 - 1.0 / TAU_FLOW
    scale = rho * (1.0 / TAU_FLOW / 36.0)
    source = push * ((1.0 - 0.5 / TAU_FLOW) / 36.0)
    base = scale * (1.0 - 1.5 * (ux * ux + uy * uy + uz * uz)) - 3.0 * source * uz
    linear, square = 3.0 * scale, 4.5 * scale
    push1, push2 = 3.0 * source, 9.0 * source
    out = [None] * COUNT
    out[0] = keep * f[0] + 12.0 * base
    for q in range(1, NFLOW, 2):
        c = LATTICE[q]
        along = None
        for axis in range(3):
            if c[axis]:
                along = u[axis] if along is None else along + u[axis] if c[axis] == 1 else along - u[axis]
        inner = square * along
        odd = linear * along
        if c[2] == 1:
            inner, odd = inner + push2, odd + push1
        elif c[2] == -1:
            inner, odd = inner - push2, odd - push1
        even = base + inner * along
        if q < 7:
            even, odd = 2.0 * even, 2.0 * odd
        out[q] = keep * f[q] + (even + odd)
        out[q + 1] = keep * f[q + 1] + (even - odd)
    keep = 1.0 - 1.0 / TAU_HEAT
    out[NFLOW] = keep * f[NFLOW] + (HEAT_WEIGHT[0] / TAU_HEAT) * temp
    rest = (HEAT_WEIGHT[1] / TAU_HEAT) * temp
    for axis in range(3):
        q = NFLOW + 1 + 2 * axis
        drift = 4.0 * rest * u[axis]
        out[q] = keep * f[q] + (rest + drift)
        out[q + 1] = keep * f[q + 1] + (rest - drift)
    return out


def parity(axis):
    return lax.axis_index(axis) % 2 == 1


def send(outs, up, down, odd, at, count):
    for j in range(len(up)):
        if len(outs) == 1:
            outs[0][at + j] = up[j]
            outs[0][count + at + j] = down[j]
        else:
            outs[0][at + j] = jnp.where(odd, down[j], up[j])
            outs[1][at + j] = jnp.where(odd, up[j], down[j])


def send_rows(outs, up, down, odd, count):
    height = outs[0].shape[1]
    for i in range(len(up)):
        t, r = divmod(i, height)
        if len(outs) == 1:
            outs[0][t, r : r + 1, :] = up[i]
            outs[0][count + t, r : r + 1, :] = down[i]
        else:
            outs[0][t, r : r + 1, :] = jnp.where(odd, down[i], up[i])
            outs[1][t, r : r + 1, :] = jnp.where(odd, up[i], down[i])


def received(ins, odd, count):
    if len(ins) == 1:
        return {1: lambda j: ins[0][j], -1: lambda j: ins[0][count + j]}
    return {
        1: lambda j: jnp.where(odd, ins[0][j], ins[1][j]),
        -1: lambda j: jnp.where(odd, ins[1][j], ins[0][j]),
    }


def swap_pairs(size, periodic=True):
    if size == 1:
        return [[(0, 0)], [(0, 0)]]
    first = [(i, i + 1) for i in range(0, size - 1, 2)]
    second = [(i, i + 1) for i in range(1, size - 1, 2)] + ([(size - 1, 0)] if periodic else [])
    return [[p for a, b in pairs for p in ((a, b), (b, a))] for pairs in (first, second)]


def swap(buffers, axis, size, periodic=True):
    if size == 1:
        return list(buffers)
    return [lax.ppermute(b, axis, route) for b, route in zip(buffers, swap_pairs(size, periodic))]


def swap_corners(buffers, nx, ny):
    moved = {}
    for way in (1, -1) if nx > 2 else (1,):
        moved[way] = []
        for b, along_y in zip(buffers, swap_pairs(ny)):
            route = [(x * ny + y, (x + way) % nx * ny + to) for x in range(nx) for y, to in along_y]
            moved[way].append(lax.ppermute(b, ("gx", "gy"), route))
    return [b for way in moved for b in moved[way]]


def call(kernel, ins, outs, flops, scratch=(), in_space=None, out_space=None, sems=0, alias=None):
    in_space = [pltpu.VMEM] * len(ins) if in_space is None else in_space
    out_space = [pltpu.VMEM] * len(outs) if out_space is None else out_space
    return pl.pallas_call(
        kernel,
        out_shape=[jax.ShapeDtypeStruct(s, jnp.float32) for s in outs],
        in_specs=[pl.BlockSpec(memory_space=s) for s in in_space],
        out_specs=[pl.BlockSpec(memory_space=s) for s in out_space],
        scratch_shapes=[pltpu.VMEM(s, jnp.float32) for s in scratch]
        + ([pltpu.SemaphoreType.DMA((sems,))] if sems else []),
        input_output_aliases=alias or {},
        compiler_params=pltpu.CompilerParams(vmem_limit_bytes=12 * 2**20),
        cost_estimate=pl.CostEstimate(flops=flops, bytes_accessed=flops // 8, transcendentals=0),
    )(*ins)


def plane_reader(refs, X):
    if len(refs) == 1:
        return lambda q, x: refs[0][q, x]
    return lambda q, x: refs[0][q, x - 1] if 0 < x < X - 1 else refs[1][q, 0 if x == 0 else 1]


def per_device(sizes, flow, heat):
    X, Y, Z = flow.shape[1:]
    slots = Z // SLOT
    half = slots // 2
    nx, ny, nz = (sizes[a] for a in ("gx", "gy", "gz"))
    assert all(n == 1 or n % 2 == 0 for n in (nx, ny, nz))
    assert STEPS > 1 and 2 * STEPS <= SLOT and 2 * STEPS <= Y and STEPS <= Z and Z % SLOT == 0
    assert slots % X == 0 and FACE <= half and X > 2 and 4 * (STEPS - 1) <= Y
    share = slots // X
    ztiles = -(-COUNT // share)
    groups = -(-COUNT // X)
    tile = (Y, Z)
    bx = 1 if nx <= 2 else 2
    by = 1 if ny <= 2 else 2
    big, ring = (COUNT, X, Y, Z), (groups * X, Y, Z)
    inner_big, outer_big = (COUNT, X - 2, Y, Z), (COUNT, 2, Y, Z)
    inner_xs, outer_xs = range(1, X - 1), (0, X - 1)

    def needed(q, j, sign):
        _, cy, cz = LATTICE[q]
        return j == 1 or cy == sign or (j < STEPS and (cy == 0 or cz != 0))

    rows = {
        sign: [(q, j) for j in range(1, STEPS + 1) for q in range(COUNT) if needed(q, j, sign)]
        for sign in (1, -1)
    }
    corner_rows = {
        sign: [
            (way, q, j)
            for way in (1, -1)
            for j in range(1, STEPS + 1)
            for q in MOVING[0, way]
            if needed(q, j, sign)
        ]
        for sign in (1, -1)
    }
    cut = len(corner_rows[1])
    ctiles = -(-(cut + 2 * STEPS) // Y)
    row_of = {1: lambda j: Y - j, -1: lambda j: j - 1}
    ymain = len(rows[1])
    ytiles = ymain + (STEPS - 1) * groups + 1
    ways = 1 if nx <= 2 else 2
    x_first, x_later = FACE + 1, FACE + FACE // 2 + 1
    yshape = [(2 * ytiles // by, X, Z)] * by
    cshape = [(2 * ctiles // by, Y, Z)] * by
    xshape = lambda n: [(2 * n // bx, Y, Z)] * bx
    climbing = MOVING[2, 1] + MOVING[2, -1]
    work = COUNT * X * Y * Z * 10

    def load(flow_ref, heat_ref, raw_ref, pack_ref, sems):
        bounds = [0, NFLOW // 2 + 1, NFLOW, COUNT]
        copies = [
            pltpu.make_async_copy(
                flow_ref.at[a:b] if a < NFLOW else heat_ref.at[a - NFLOW : b - NFLOW],
                raw_ref.at[a:b],
                sems.at[i],
            )
            for i, (a, b) in enumerate(zip(bounds, bounds[1:]))
        ]
        for copy in copies:
            copy.start()
        lane = lanes_of(tile)
        for t in range(ztiles):
            packed = None
            for k, q in enumerate(range(t * share, min((t + 1) * share, COUNT))):
                if q in bounds:
                    copies[bounds.index(q)].wait()
                for x in range(X):
                    slot = k * X + x
                    moved = roll(raw_ref[q, x], STEPS + SLOT * slot, 1)
                    packed = moved if slot == 0 else jnp.where(lane >= SLOT * slot, moved, packed)
            pack_ref[t] = packed

    def first_main(raw_ref, post_ref, *y_refs):
        for x in range(X):
            for q, value in enumerate(collide([raw_ref[q, x] for q in range(COUNT)])):
                post_ref[q, x] = value
        send(y_refs, *(y_rows(post_ref, sign) for sign in (1, -1)), parity("gy"), 0, ytiles)

    def y_rows(post_ref, sign):
        return [post_ref[q, :, row_of[sign](j), :] for q, j in rows[sign]]

    def pack_rings(rings, sign):
        lane, packed = lanes_of(tile), None
        for i, ring_ref in enumerate(rings):
            for j, q in enumerate(MOVING[0, sign]):
                to = i * half + j
                moved = roll(ring_ref[q], SLOT * (to - (X - 1 if sign == 1 else 0)), 1)
                packed = moved if packed is None else jnp.where(lane >= SLOT * to, moved, packed)
        return packed

    def first_halo(za_ref, zb_ref, post_ref, *refs):
        y_before, refs = refs[:by], refs[by:]
        ring_ref, x_outs, refs = refs[0], refs[1 : 1 + bx], refs[1 + bx :]
        y_outs, corner_outs, packed_ref = refs[:by], refs[by : 2 * by], refs[2 * by]
        odd = parity("gz")
        inside = lanes_of(tile) % SLOT < STEPS
        f = []
        for t in range(ztiles):
            a, b = za_ref[t], zb_ref[t]
            merged = jnp.where(inside, jnp.where(odd, a, b), jnp.where(odd, b, a))
            for k, q in enumerate(range(t * share, min((t + 1) * share, COUNT))):
                f.append(roll(merged, -k * X * SLOT, 1))
        for q, value in enumerate(collide(f)):
            ring_ref[q] = value
        for q in range(COUNT, groups * X):
            ring_ref[q] = jnp.zeros(tile, jnp.float32)
        faces = []
        for i, (way, x) in enumerate(((1, X - 1), (-1, 0))):
            packed = pack_rings([ring_ref], way)
            packed_ref[i] = packed
            faces.append([post_ref[q, x] for q in MOVING[0, way]] + [packed])
        send(x_outs, faces[0], faces[1], parity("gx"), 0, x_first)
        odd = parity("gy")
        faces, corners = [], []
        for sign in (1, -1):
            at = row_of[sign]
            tiles = [
                ring_ref[g * X : (g + 1) * X, at(j), :] for j in range(1, STEPS) for g in range(groups)
            ]
            last = None
            for k, q in enumerate(MOVING[1, sign]):
                row = spread(ring_ref[q, at(STEPS) : at(STEPS) + 1, :], (X, Z))
                last = row if k == 0 else jnp.where(rows_of((X, Z)) == k, row, last)
            faces.append(tiles + [last])
            corners.append(
                [
                    post_ref[q, X - 1 if way == 1 else 0, at(j) : at(j) + 1, :]
                    for way, q, j in corner_rows[sign]
                ]
                + [packed_ref[i, at(j) : at(j) + 1, :] for i in (0, 1) for j in range(1, STEPS + 1)]
            )
        send(y_outs, faces[0], faces[1], odd, ymain, ytiles)
        send_rows(corner_outs, corners[0], corners[1], odd, ctiles)

    def edges_first(x_refs, corner_refs, edge_ref):
        odd_y = parity("gy")
        from_x = received(x_refs, parity("gx"), x_first)
        for i, way in enumerate((1, -1)):
            refs = corner_refs[:by] if way == 1 or ways == 1 else corner_refs[by:]
            for sign in (1, -1):
                at = row_of[sign]
                entries = [
                    (i * FACE + MOVING[0, way].index(q), j, n)
                    for n, (w, q, j) in enumerate(corner_rows[sign])
                    if w == way
                ] + [(2 * FACE + i, j, cut + i * STEPS + j - 1) for j in range(1, STEPS + 1)]
                for to, j, n in entries:
                    t, r = divmod(n, Y)
                    if by == 1:
                        row = refs[0][t if sign == 1 else ctiles + t, r : r + 1, :]
                    else:
                        a, b = refs[0][t, r : r + 1, :], refs[1][t, r : r + 1, :]
                        row = jnp.where(odd_y, a, b) if sign == 1 else jnp.where(odd_y, b, a)
                    edge_ref[to, at(j) : at(j) + 1, :] = row
        ring_tiles = {
            1: (from_x[1](FACE), edge_ref[2 * FACE]),
            -1: (from_x[-1](FACE), edge_ref[2 * FACE + 1]),
        }

        def around(cx, j):
            return edge_ref[j if cx == 1 else FACE + j]

        def ring_edge(cx, j, i):
            return roll(ring_tiles[cx][i], SLOT * ((0 if cx == 1 else X - 1) - j), 1)

        return (lambda cx, j: from_x[cx](j)), around, ring_edge

    def edges_later(x_refs):
        from_x = received(x_refs, parity("gx"), x_later)
        ring_tiles = {cx: from_x[cx](x_later - 1) for cx in (1, -1)}

        def around(cx, j):
            t = from_x[cx](FACE + j // 2)
            return roll(t, Y // 2, 0) if j % 2 else t

        def ring_edge(cx, j, i):
            return roll(ring_tiles[cx], SLOT * ((0 if cx == 1 else X - 1) - i * half - j), 1)

        return (lambda cx, j: from_x[cx](j)), around, ring_edge

    def send_later(outs, main, side, rings):
        sub = rows_of(tile)
        near = (sub < Y // 4) | (sub >= Y - Y // 4)
        faces = []
        for sign, x in ((1, X - 1), (-1, 0)):
            moving = MOVING[0, sign]
            pairs = [
                jnp.where(near, side(a, x), roll(side(b, x), Y // 2, 0))
                for a, b in zip(moving[::2], moving[1::2])
            ]
            faces.append([main(q, x) for q in moving] + pairs + [pack_rings(rings, sign)])
        send(outs, faces[0], faces[1], parity("gx"), 0, x_later)

    def stream(main, side, rings, edges, xs, put, put_ring, grown_refs=None, last=False, done=None):
        lane, sub = lanes_of(tile), rows_of(tile)
        ends = {1: lane == 0, -1: lane == Z - 1}
        on_wall = {
            1: ends[1] & (lax.axis_index("gz") == 0),
            -1: ends[-1] & (lax.axis_index("gz") == nz - 1),
        }
        borders = {1: sub == 0, -1: sub == Y - 1}
        x_slot = {1: lane < SLOT, -1: lane >= SLOT * (X - 1)}
        edge_main, edge_side, edge_ring = edges if edges else (None, None, None)

        def along_y(t, u, cy):
            if not cy:
                return t, u
            t, u = roll(t, cy, 0), roll(u, cy, 0)
            return jnp.where(borders[cy], u, t), jnp.where(borders[cy], t, u)

        for q in range(COUNT):
            cx, cy, cz = LATTICE[q]
            around = grown = None
            if cz or put_ring:
                around = [rings[0][q], rings[1][q]]
                if cx:
                    around = [roll(t, SLOT * cx, 1) for t in around]
                    if edges:
                        j = MOVING[0, cx].index(q)
                        around = [
                            jnp.where(x_slot[cx], edge_ring(cx, j, i), t) for i, t in enumerate(around)
                        ]
                around = along_y(*around, cy)
                grown = around
            if cz and put_ring:
                grown = [roll(t, cz, 1) for t in around]
                if grown_refs:
                    far = STEPS if cz == 1 else STEPS - 1
                    other = (lane % SLOT == far) & (lane >= SLOT) & (lane < SLOT * (X - 1))
                    i = climbing.index(q)
                    grown = [jnp.where(other, ref[i], t) for ref, t in zip(grown_refs, grown)]
            for x in xs:
                if 0 <= x - cx < X:
                    t, u = main(q, x - cx), side(q, x - cx) if cy or not last else None
                else:
                    j = MOVING[0, cx].index(q)
                    t, u = edge_main(cx, j), edge_side(cx, j) if cy or not last else None
                t, u = along_y(t, u, cy)
                if cz:
                    near = SLOT * x + (STEPS - 1 if cz == 1 else STEPS)
                    far = SLOT * x + (STEPS if cz == 1 else STEPS - 1)
                    end = 0 if cz == 1 else Z - 1
                    if put_ring:
                        grown = [
                            jnp.where(lane == far, roll(v, far - end + cz, 1), g)
                            for v, g in zip((t, u), grown)
                        ]

                    def along_z(v, beside, plane):
                        back = plane(OPPOSITE[q], x)
                        if q >= NFLOW:
                            wall = HOT_WALL if cz == 1 else COLD_WALL
                            back = 2.0 * HEAT_WEIGHT[q - NFLOW] * wall - back
                        v = jnp.where(ends[cz], roll(beside, end - near, 1), roll(v, cz, 1))
                        return jnp.where(on_wall[cz], back, v)

                    t = along_z(t, around[0], main)
                    u = None if last else along_z(u, around[1], side)
                put(q, x, t, u)
            if put_ring:
                put_ring(q, grown)
            if done:
                done(q)

    def collide_in(ref, planes):
        for x in planes:
            for q, value in enumerate(collide([ref[q, x] for q in range(COUNT)])):
                ref[q, x] = value

    def collide_ring(ref):
        for q, value in enumerate(collide([ref[q] for q in range(COUNT)])):
            ref[q] = value

    def putter(main_ref, side_ref, at):
        def put(q, x, t, u):
            main_ref[q, at(x)] = t
            if side_ref is not None:
                side_ref[q, at(x)] = u

        return put

    def ring_putter(refs):
        def put_ring(q, values):
            for ref, value in zip(refs, values):
                ref[q] = value

        return put_ring

    def first_step(post_ref, ring_ref, *refs):
        x_refs, refs = refs[:bx], refs[bx:]
        y_refs, refs = refs[:by], refs[by:]
        corner_refs, refs = refs[: by * ways], refs[by * ways :]
        new_ref, new_side, new_ring, new_ring_side = refs[:4]
        outs, side_ref, ring_side, edge_ref = refs[4:-3], refs[-3], refs[-2], refs[-1]
        from_y = received(y_refs, parity("gy"), ytiles)
        for sign in (1, -1):
            at = row_of[sign]
            for i, (q, j) in enumerate(rows[sign]):
                side_ref[q, :, at(j), :] = from_y[sign](i)
            i = ymain
            for j in range(1, STEPS):
                for g in range(groups):
                    ring_side[g * X : (g + 1) * X, at(j), :] = from_y[sign](i)
                    i += 1
            last = from_y[sign](i)
            for k, q in enumerate(MOVING[1, sign]):
                ring_side[q, at(STEPS) : at(STEPS) + 1, :] = last[k : k + 1, :]
        main, side = plane_reader([post_ref], X), plane_reader([side_ref], X)
        edges = edges_first(x_refs, corner_refs, edge_ref)
        put = putter(new_ref, new_side, lambda x: x)
        put_ring = ring_putter((new_ring, new_ring_side))
        stream(main, side, (ring_ref, ring_side), edges, range(X), put, put_ring)
        for ref in (new_ref, new_side):
            collide_in(ref, range(X))
        for ref in (new_ring, new_ring_side):
            collide_ring(ref)
        main, side = plane_reader([new_ref], X), plane_reader([new_side], X)
        send_later(outs, main, side, (new_ring, new_ring_side))

    def state_of(refs, parts):
        main = plane_reader(refs[:parts], X)
        side = plane_reader(refs[parts : 2 * parts], X)
        return main, side, refs[2 * parts : 2 * parts + 2], refs[2 * parts + 2 :]

    def inner_step(parts, *refs):
        main, side, rings, refs = state_of(refs, parts)
        new_ref, new_side, grown_ref, grown_side = refs

        def put_ring(q, values):
            if q in climbing:
                grown_ref[climbing.index(q)] = values[0]
                grown_side[climbing.index(q)] = values[1]

        put = putter(new_ref, new_side, lambda x: x - 1)
        stream(main, side, rings, None, inner_xs, put, put_ring)
        for ref in (new_ref, new_side):
            collide_in(ref, range(X - 2))

    def outer_step(parts, *refs):
        main, side, rings, refs = state_of(refs, parts)
        x_refs, refs = refs[:bx], refs[bx:]
        grown_refs, refs = refs[:2], refs[2:]
        new_ref, new_side, new_ring, new_ring_side = refs[:4]
        outs = refs[4:]
        put = putter(new_ref, new_side, lambda x: 0 if x == 0 else 1)
        put_ring = ring_putter((new_ring, new_ring_side))
        edges = edges_later(x_refs)
        stream(main, side, rings, edges, outer_xs, put, put_ring, grown_refs)
        for ref in (new_ref, new_side):
            collide_in(ref, range(2))
        for ref in (new_ring, new_ring_side):
            collide_ring(ref)
        at = lambda ref: lambda q, x: ref[q, 0 if x == 0 else 1]
        send_later(outs, at(new_ref), at(new_side), (new_ring, new_ring_side))

    def flux(ref, planes):
        parts = []
        for x in planes:
            _, temp, _, _, _, uz = moments([ref[q, x] for q in range(COUNT)])
            parts.append(uz * temp)
        return total_of(parts)

    def copies_of(source, flow_ref, heat_ref, where, sems):
        return [
            pltpu.make_async_copy(source.at[a:b], ref.at[:, where], sem)
            for ref, a, b, sem in zip((flow_ref, heat_ref), (0, NFLOW), (NFLOW, COUNT), sems)
        ]

    def inner_last(parts, *refs):
        main, side, rings, refs = state_of(refs, parts)
        flow_ref, heat_ref, part_ref, new_ref, sems = refs
        put = putter(new_ref, None, lambda x: x - 1)
        stream(main, side, rings, None, inner_xs, put, None, last=True)
        copies = copies_of(new_ref, flow_ref, heat_ref, slice(1, X - 1), [sems.at[0], sems.at[1]])
        for copy in copies:
            copy.start()
        part_ref[...] = flux(new_ref, range(X - 2))
        for copy in copies:
            copy.wait()

    devices = nx * ny * nz

    def outer_last(parts, *refs):
        main, side, rings, refs = state_of(refs, parts)
        x_refs, (inner_part, new_ref, part_ref) = refs[:bx], refs[bx:]
        put = putter(new_ref, None, lambda x: 0 if x == 0 else 1)
        stream(main, side, rings, edges_later(x_refs), outer_xs, put, None, last=True)
        part = jnp.sum(flux(new_ref, range(2)) + inner_part[...], axis=0, keepdims=True)
        part_ref[...] = jnp.broadcast_to(part[None], part_ref.shape)

    cells = X * Y * Z * devices
    factor = Z * nz / (DIFFUSIVITY * (HOT_WALL - COLD_WALL)) / cells

    def finish(parts_ref, outer_ref, flow_in, heat_in, flow_ref, heat_ref, out_ref, number, sems):
        copies = []
        for i, x in enumerate(outer_xs):
            copies += copies_of(
                outer_ref.at[:, i], flow_ref, heat_ref, x, [sems.at[2 * i], sems.at[2 * i + 1]]
            )
        for copy in copies:
            copy.start()
        part = jnp.sum(parts_ref[...], axis=0)
        number[...] = 1.0 + factor * jnp.sum(part, axis=1, keepdims=True)
        copies.append(pltpu.make_async_copy(number, out_ref, sems.at[4]))
        copies[-1].start()
        for copy in copies:
            copy.wait()

    flow, heat = (pltpu.with_memory_space_constraint(a, pltpu.HBM) for a in (flow, heat))
    raw, zpack = call(
        load, (flow, heat), [big, (ztiles, Y, Z)], work, in_space=[pltpu.HBM] * 2, sems=3
    )
    za, zb = swap([zpack, zpack], "gz", nz, False)
    post, *ys = call(first_main, (raw,), [big] + yshape, 20 * work)
    around, *buffers = call(
        first_halo,
        (za, zb, post, *ys),
        [ring] + xshape(x_first) + yshape + cshape,
        2 * work,
        [(2, Y, Z)],
        alias={3 + i: 1 + bx + i for i in range(by)},
    )
    xs, ys, corners = buffers[:bx], buffers[bx : bx + by], buffers[bx + by :]
    moved = [*swap(xs, "gx", nx), *swap(ys, "gy", ny), *swap_corners(corners, nx, ny)]
    main, side, ring_main, ring_side, *xs = call(
        first_step,
        (post, around, *moved),
        [big, big, ring, ring] + xshape(x_later),
        40 * work,
        [big, ring, (2 * FACE + 2, Y, Z)],
    )
    main, side = [main], [side]
    grown_shape = (len(climbing), Y, Z)
    for _ in range(STEPS - 2):
        state = (*main, *side, ring_main, ring_side)
        xs = swap(xs, "gx", nx)
        inner, inner_side, *grown = call(
            functools.partial(inner_step, len(main)),
            state,
            [inner_big, inner_big, grown_shape, grown_shape],
            40 * work,
        )
        outer, outer_side, ring_main, ring_side, *xs = call(
            functools.partial(outer_step, len(main)),
            (*state, *xs, *grown),
            [outer_big, outer_big, ring, ring] + xshape(x_later),
            10 * work,
        )
        main, side = [inner, outer], [inner_side, outer_side]
    state = (*main, *side, ring_main, ring_side)
    xs = swap(xs, "gx", nx)
    flow, heat, inner_part = call(
        functools.partial(inner_last, len(main)),
        state,
        [flow.shape, heat.shape, tile],
        40 * work,
        [inner_big],
        out_space=[pltpu.HBM, pltpu.HBM, pltpu.VMEM],
        sems=2,
    )
    outer, parts = call(
        functools.partial(outer_last, len(main)),
        (*state, *xs, inner_part),
        [outer_big, (devices, 1, Z)],
        10 * work,
    )
    parts = lax.all_to_all(parts, ("gx", "gy", "gz"), 0, 0, tiled=True)
    flow, heat, nusselt = call(
        finish,
        (parts, outer, flow, heat),
        [flow.shape, heat.shape, (1, 1)],
        work,
        [(1, 1)],
        in_space=[pltpu.VMEM, pltpu.VMEM, pltpu.HBM, pltpu.HBM],
        out_space=[pltpu.HBM, pltpu.HBM, pltpu.HBM],
        sems=5,
        alias={2: 0, 3: 1},
    )
    return flow, heat, nusselt.reshape(())


def solution(mesh):
    placed = P(None, "gx", "gy", "gz")
    return jax.shard_map(
        functools.partial(per_device, dict(mesh.shape)),
        mesh=mesh,
        in_specs=(placed, placed),
        out_specs=(placed, placed, P()),
        check_vma=False,
    )
```

time: 47.5 us -> 43.5 us (0.916)
  starting transfers between devices: 21.2 us -> 14.6 us
  Pallas kernels: 4.72 us -> 7.72 us
  local copies, waits for them, and re-layouts: 2.01 us -> 0 us
  blocking collectives: 10.4 us -> 11.3 us
  waiting for transfers between devices: 8.19 us -> 9.02 us
    ppermute x17 -> x9, starting transfers between devices: 21.2 us -> 14.6 us  [the longest x7 12.9 us: swap(): lax.ppermute(b, axis, route)]
    pallas_call x7 -> x9, Pallas kernels: 4.72 us -> 7.72 us  [call(): pl.pallas_call(kernel, out_shape=[jax.ShapeDtypeStruct(s, jnp.float32) fo...]
    unnamed x4 -> x0, local copies, waits for them, and re-layouts: 2.01 us -> none
    all_to_all x1, blocking collectives: 10.4 us -> 11.3 us  [per_device(): parts = lax.all_to_all(parts, ('gx', 'gy', 'gz'), 0, 0, tiled=True)]
    ppermute x17 -> x9, waiting for transfers between devices: 8.19 us -> 9.02 us  [the longest x7 6.54 us: swap(): lax.ppermute(b, axis, route)]
  transfers between devices with their start and end apart: 17 -> 9, of which waited for: 7 -> 6; matrix products, arithmetic and copies ran while one was open for 0% -> 0% of each run, Pallas kernels for 1% -> 7%
where the time goes in v3:
time: 43.5 us; the launch traced here: 43.3 us
  starting transfers between devices  14.6 us (34%)
  blocking collectives  11.3 us (26%)
  waiting for transfers between devices  9.02 us (21%)
  Pallas kernels  7.72 us (18%)
  between operations  0.72 us (2%)
    ppermute x7, starting transfers between devices, swap(): lax.ppermute(b, axis, route)  12.9 us
    all_to_all x1, blocking collectives, per_device(): parts = lax.all_to_all(parts, ('gx', 'gy', 'gz'), 0, 0, tiled=True)  11.3 us
    pallas_call x9, Pallas kernels, call(): pl.pallas_call(kernel, out_shape=[jax.ShapeDtypeStruct(s, jnp.float32) fo...  7.72 us
    ppermute x7, waiting for transfers between devices, swap(): lax.ppermute(b, axis, route)  6.54 us
    ppermute x2, waiting for transfers between devices, swap_corners(): moved[way].append(lax.ppermute(b, ('gx', 'gy'), route))  2.48 us
    ppermute x2, starting transfers between devices, swap_corners(): moved[way].append(lax.ppermute(b, ('gx', 'gy'), route))  1.69 us
  transfers between devices with their start and end apart: 9, of which 6 were waited for; matrix products, arithmetic and copies ran while one was open for 0% of the time, Pallas kernels for 7%

profile of v3, /device:TPU:0, one launch (start us, length us, event | category | flops | bytes accessed | tf_op | source)
XLA Modules:
  0.0 43.3 jit_solution(7354238035659626021)
XLA Ops:
  0.6 1.4 %shard_map.49 = (f32[26,8,8,128]{3,2,1,0:T(8,128)S(1)}, f32[13,8,128]{2,1,0:T(8,128)S(1)}) custom-call(f32[19,8,8,128]{3,2,1,0:T(8,128)} %flow_ref.1, f32[7,8,8,128]{3,2,1,0:T(8,128)} %heat_ref.1), custom_call_target="tpu_custom_call" | custom-call | flops 2129920 | bytes 266240 | tf_op jit(solution)/shard_map/pallas_call | solution.py:197
  2.1 0.7 %collective-permute-start.1 = (f32[13,8,128]{2,1,0:T(8,128)S(1)}, f32[13,8,128]{2,1,0:T(8,128)S(1)}, u32[]{:S(2)}, u32[]{:S(2)}) collective-permute-start(f32[13,8,128]{2,1,0:T(8,128)S(1)} %get-tuple-element.38), channel_id=1, source_target_pairs={{1,2},{2,1},{5,6},{6,5},{9,10},{10,9},{13,14},{14,13},{17,18},{18,... | collective-permute-start | bytes 159752 | tf_op jit(solution)/shard_map/ppermute | solution.py:181
  2.7 5.9 %collective-permute-start = (f32[13,8,128]{2,1,0:T(8,128)S(1)}, f32[13,8,128]{2,1,0:T(8,128)S(1)}, u32[]{:S(2)}, u32[]{:S(2)}) collective-permute-start(f32[13,8,128]{2,1,0:T(8,128)S(1)} %get-tuple-element.38), channel_id=1, source_target_pairs={{0,1},{1,0},{2,3},{3,2},{4,5},{5,4},{6,7},{7,6},{8,9},{9,8},{10,11... | collective-permute-start | bytes 159752 | tf_op jit(solution)/shard_map/ppermute | solution.py:181
  8.7 0.6 %shard_map.50 = (f32[26,8,8,128]{3,2,1,0:T(8,128)S(1)}, f32[63,8,128]{2,1,0:T(8,128)S(1)}, f32[63,8,128]{2,1,0:T(8,128)S(1)}) custom-call(f32[26,8,8,128]{3,2,1,0:T(8,128)S(1)} %get-tuple-element.36.raw_ref), custom_call_target="tpu_custom_call" | custom-call | flops 42598400 | bytes 5324800 | tf_op jit(solution)/shard_map/pallas_call | solution.py:197
  9.3 0.0 collective-permute-done.1.zb_ref
  9.3 1.5 %collective-permute-done.za_ref = f32[13,8,128]{2,1,0:T(8,128)S(1)} collective-permute-done((f32[13,8,128]{2,1,0:T(8,128)S(1)}, f32[13,8,128]{2,1,0:T(8,128)S(1)}, u32[]{:S(2)}, u32[]{:S(2)}) %collective-permute-start) | collective-permute-done | bytes 53280 | tf_op jit(solution)/shard_map/ppermute | solution.py:181
  10.8 0.2 shard_map.51
  11.0 0.1 collective-permute-start.3
  11.1 1.6 %collective-permute-start.4 = (f32[63,8,128]{2,1,0:T(8,128)S(1)}, f32[63,8,128]{2,1,0:T(8,128)S(1)}, u32[]{:S(2)}, u32[]{:S(2)}) collective-permute-start(f32[63,8,128]{2,1,0:T(8,128)S(1)} %get-tuple-element.44), channel_id=1, source_target_pairs={{4,8},{8,4},{12,0},{0,12},{5,9},{9,5},{13,1},{1,13},{6,10},{10,6},... | collective-permute-start | bytes 774152 | tf_op jit(solution)/shard_map/ppermute | solution.py:181
  12.7 1.5 %collective-permute-start.2 = (f32[14,8,128]{2,1,0:T(8,128)S(1)}, f32[14,8,128]{2,1,0:T(8,128)S(1)}, u32[]{:S(2)}, u32[]{:S(2)}) collective-permute-start(f32[14,8,128]{2,1,0:T(8,128)S(1)} %get-tuple-element.42), channel_id=1, source_target_pairs={{0,16},{16,0},{1,17},{17,1},{2,18},{18,2},{3,19},{19,3},{4,20},{20... | collective-permute-start | bytes 172040 | tf_op jit(solution)/shard_map/ppermute | solution.py:181
  14.2 0.0 collective-permute-start.5
  14.2 1.7 %collective-permute-start.6 = (f32[4,8,128]{2,1,0:T(8,128)S(1)}, f32[4,8,128]{2,1,0:T(8,128)S(1)}, u32[]{:S(2)}, u32[]{:S(2)}) collective-permute-start(f32[4,8,128]{2,1,0:T(8,128)S(1)} %get-tuple-element.46), channel_id=1, source_target_pairs={{4,24},{8,20},{12,16},{0,28},{20,8},{24,4},{28,0},{16,12},{5,25},{... | collective-permute-start | bytes 49160 | tf_op jit(solution)/shard_map/ppermute | solution.py:190
  15.9 1.6 %collective-permute-done.5.refs_3_ = f32[4,8,128]{2,1,0:T(8,128)S(1)} collective-permute-done((f32[4,8,128]{2,1,0:T(8,128)S(1)}, f32[4,8,128]{2,1,0:T(8,128)S(1)}, u32[]{:S(2)}, u32[]{:S(2)}) %collective-permute-start.5) | collective-permute-done | bytes 16416 | tf_op jit(solution)/shard_map/ppermute | solution.py:190
  17.5 0.9 %collective-permute-done.6.refs_4_ = f32[4,8,128]{2,1,0:T(8,128)S(1)} collective-permute-done((f32[4,8,128]{2,1,0:T(8,128)S(1)}, f32[4,8,128]{2,1,0:T(8,128)S(1)}, u32[]{:S(2)}, u32[]{:S(2)}) %collective-permute-start.6) | collective-permute-done | bytes 16416 | tf_op jit(solution)/shard_map/ppermute | solution.py:190
  18.4 0.0 collective-permute-done.2.refs_0_
  18.4 0.0 collective-permute-done.3.refs_1_
  18.4 1.0 %collective-permute-done.4.refs_2_ = f32[63,8,128]{2,1,0:T(8,128)S(1)} collective-permute-done((f32[63,8,128]{2,1,0:T(8,128)S(1)}, f32[63,8,128]{2,1,0:T(8,128)S(1)}, u32[]{:S(2)}, u32[]{:S(2)}) %collective-permute-start.4) | collective-permute-done | bytes 258080 | tf_op jit(solution)/shard_map/ppermute | solution.py:181
  19.4 1.7 %shard_map.52 = (f32[26,8,8,128]{3,2,1,0:T(8,128)S(1)}, f32[26,8,8,128]{3,2,1,0:T(8,128)S(1)}, f32[32,8,128]{2,1,0:T(8,128)S(1)}, f32[32,8,128]{2,1,0:T(8,128)S(1)}, f32[20,8,128]{2,1,0:T(8,128)S(1)}) custom-call(f32[26,8,8,128]{3,2,1,0:T(8,128)S(1)} %get-tuple-element.37.post_ref, f32[32,8,128]{2,1,0:T(8,128)S(1)} %get-tuple-element.41.ring_ref, ...), custom_call_target="tpu_custom_call" | custom-call | flops 85196800 | bytes 10649600 | tf_op jit(solution)/shard_map/pallas_call | solution.py:197
  21.1 1.6 %collective-permute-start.7 = (f32[20,8,128]{2,1,0:T(8,128)S(1)}, f32[20,8,128]{2,1,0:T(8,128)S(1)}, u32[]{:S(2)}, u32[]{:S(2)}) collective-permute-start(f32[20,8,128]{2,1,0:T(8,128)S(1)} %get-tuple-element.52), channel_id=1, source_target_pairs={{0,16},{16,0},{1,17},{17,1},{2,18},{18,2},{3,19},{19,3},{4,20},{20... | collective-permute-start | bytes 245768 | tf_op jit(solution)/shard_map/ppermute | solution.py:181
  22.6 1.1 %shard_map.53 = (f32[26,6,8,128]{3,2,1,0:T(8,128)S(1)}, f32[26,6,8,128]{3,2,1,0:T(8,128)S(1)}, f32[12,8,128]{2,1,0:T(8,128)S(1)}, f32[12,8,128]{2,1,0:T(8,128)S(1)}) custom-call(f32[26,8,8,128]{3,2,1,0:T(8,128)S(1)} %get-tuple-element.47.refs_0_, f32[26,8,8,128]{3,2,1,0:T(8,128)S(1)} %get-tuple-element.48.refs_1_, ...), custom_call_target="tpu_custom_call" | custom-call | flops 85196800 | bytes 10649600 | tf_op jit(solution)/shard_map/pallas_call | solution.py:197
  23.7 2.2 %collective-permute-done.7.refs_4_ = f32[20,8,128]{2,1,0:T(8,128)S(1)} collective-permute-done((f32[20,8,128]{2,1,0:T(8,128)S(1)}, f32[20,8,128]{2,1,0:T(8,128)S(1)}, u32[]{:S(2)}, u32[]{:S(2)}) %collective-permute-start.7) | collective-permute-done | bytes 81952 | tf_op jit(solution)/shard_map/ppermute | solution.py:181
  25.9 0.7 %shard_map.54 = (f32[26,2,8,128]{3,2,1,0:T(8,128)S(1)}, f32[26,2,8,128]{3,2,1,0:T(8,128)S(1)}, f32[32,8,128]{2,1,0:T(8,128)S(1)}, f32[32,8,128]{2,1,0:T(8,128)S(1)}, f32[20,8,128]{2,1,0:T(8,128)S(1)}) custom-call(f32[26,8,8,128]{3,2,1,0:T(8,128)S(1)} %get-tuple-element.47.refs_0_, f32[26,8,8,128]{3,2,1,0:T(8,128)S(1)} %get-tuple-element.48.refs_1_, ...), custom_call_target="tpu_custom_call" | custom-call | flops 21299200 | bytes 2662400 | tf_op jit(solution)/shard_map/pallas_call | solution.py:197
  26.6 1.6 %collective-permute-start.8 = (f32[20,8,128]{2,1,0:T(8,128)S(1)}, f32[20,8,128]{2,1,0:T(8,128)S(1)}, u32[]{:S(2)}, u32[]{:S(2)}) collective-permute-start(f32[20,8,128]{2,1,0:T(8,128)S(1)} %get-tuple-element.60), channel_id=1, source_target_pairs={{0,16},{16,0},{1,17},{17,1},{2,18},{18,2},{3,19},{19,3},{4,20},{20... | collective-permute-start | bytes 245768 | tf_op jit(solution)/shard_map/ppermute | solution.py:181
  28.2 1.1 %shard_map.55 = (f32[19,8,8,128]{3,2,1,0:T(8,128)}, f32[7,8,8,128]{3,2,1,0:T(8,128)}, f32[8,128]{1,0:T(8,128)S(1)}) custom-call(f32[26,6,8,128]{3,2,1,0:T(8,128)S(1)} %get-tuple-element.51.refs_0_, f32[26,2,8,128]{3,2,1,0:T(8,128)S(1)} %get-tuple-element.55.refs_1_, f32[26,6,8,128]{3,2,1,0:T(8,128)S(1)} %get-tuple-element.56.refs_2_, ...), custom_call_target="tpu_custom_call" | custom-call | flops 85196800 | bytes 10649600 | tf_op jit(solution)/shard_map/pallas_call | solution.py:197
  29.3 1.8 %collective-permute-done.8.refs_6_ = f32[20,8,128]{2,1,0:T(8,128)S(1)} collective-permute-done((f32[20,8,128]{2,1,0:T(8,128)S(1)}, f32[20,8,128]{2,1,0:T(8,128)S(1)}, u32[]{:S(2)}, u32[]{:S(2)}) %collective-permute-start.8) | collective-permute-done | bytes 81952 | tf_op jit(solution)/shard_map/ppermute | solution.py:181
  31.1 0.2 shard_map.56
  31.3 11.3 %all_to_all.5.parts_ref = f32[32,1,128]{2,1,0:T(1,128)S(1)} all-to-all(f32[32,1,128]{2,1,0:T(1,128)S(1)} %get-tuple-element.62), channel_id=1, replica_groups=mesh['gx'=2,'gy'=4,'gz'=4] {'gx','gy','gz'}, dimensions={0} | all-to-all | bytes 32768 | tf_op jit(solution)/shard_map/all_to_all | solution.py:683
  42.6 0.7 %shard_map.57 = (f32[19,8,8,128]{3,2,1,0:T(8,128)}, f32[7,8,8,128]{3,2,1,0:T(8,128)}, f32[1,1]{1,0:T(1,128)}) custom-call(f32[32,1,128]{2,1,0:T(1,128)S(1)} %all_to_all.5.parts_ref, f32[26,2,8,128]{3,2,1,0:T(8,128)S(1)} %get-tuple-element.63.outer_ref, f32[19,8,8,128]{3,2,1,0:T(8,128)} %get-tuple-element.64.flow_in, ...), custom_call_target="tpu_custom_call", output_to_operand_aliasing={{0}: (2, {}), {1}: (3, {})} | custom-call | flops 2129920 | bytes 266240 | tf_op jit(solution)/shard_map/pallas_call | solution.py:197
Async XLA Ops:
  2.1 7.2 %collective-permute-start.1 = (f32[13,8,128]{2,1,0:T(8,128)S(1)}, f32[13,8,128]{2,1,0:T(8,128)S(1)}, u32[]{:S(2)}, u32[]{:S(2)}) collective-permute-start(f32[13,8,128]{2,1,0:T(8,128)S(1)} %get-tuple-element.38), channel_id=1, source_target_pairs={{1,2},{2,1},{5,6},{6,5},{9,10},{10,9},{13,14},{14,13},{17,18},{18,... | collective-permute-start | bytes 159752 | tf_op jit(solution)/shard_map/ppermute | solution.py:181
  2.7 8.1 %collective-permute-start = (f32[13,8,128]{2,1,0:T(8,128)S(1)}, f32[13,8,128]{2,1,0:T(8,128)S(1)}, u32[]{:S(2)}, u32[]{:S(2)}) collective-permute-start(f32[13,8,128]{2,1,0:T(8,128)S(1)} %get-tuple-element.38), channel_id=1, source_target_pairs={{0,1},{1,0},{2,3},{3,2},{4,5},{5,4},{6,7},{7,6},{8,9},{9,8},{10,11... | collective-permute-start | bytes 159752 | tf_op jit(solution)/shard_map/ppermute | solution.py:181
  11.0 7.4 %collective-permute-start.3 = (f32[63,8,128]{2,1,0:T(8,128)S(1)}, f32[63,8,128]{2,1,0:T(8,128)S(1)}, u32[]{:S(2)}, u32[]{:S(2)}) collective-permute-start(f32[63,8,128]{2,1,0:T(8,128)S(1)} %get-tuple-element.43), channel_id=1, source_target_pairs={{0,4},{4,0},{8,12},{12,8},{1,5},{5,1},{9,13},{13,9},{2,6},{6,2},{1... | collective-permute-start | bytes 774152 | tf_op jit(solution)/shard_map/ppermute | solution.py:181
  11.1 8.3 %collective-permute-start.4 = (f32[63,8,128]{2,1,0:T(8,128)S(1)}, f32[63,8,128]{2,1,0:T(8,128)S(1)}, u32[]{:S(2)}, u32[]{:S(2)}) collective-permute-start(f32[63,8,128]{2,1,0:T(8,128)S(1)} %get-tuple-element.44), channel_id=1, source_target_pairs={{4,8},{8,4},{12,0},{0,12},{5,9},{9,5},{13,1},{1,13},{6,10},{10,6},... | collective-permute-start | bytes 774152 | tf_op jit(solution)/shard_map/ppermute | solution.py:181
  12.7 5.7 %collective-permute-start.2 = (f32[14,8,128]{2,1,0:T(8,128)S(1)}, f32[14,8,128]{2,1,0:T(8,128)S(1)}, u32[]{:S(2)}, u32[]{:S(2)}) collective-permute-start(f32[14,8,128]{2,1,0:T(8,128)S(1)} %get-tuple-element.42), channel_id=1, source_target_pairs={{0,16},{16,0},{1,17},{17,1},{2,18},{18,2},{3,19},{19,3},{4,20},{20... | collective-permute-start | bytes 172040 | tf_op jit(solution)/shard_map/ppermute | solution.py:181
  14.2 3.3 %collective-permute-start.5 = (f32[4,8,128]{2,1,0:T(8,128)S(1)}, f32[4,8,128]{2,1,0:T(8,128)S(1)}, u32[]{:S(2)}, u32[]{:S(2)}) collective-permute-start(f32[4,8,128]{2,1,0:T(8,128)S(1)} %get-tuple-element.45), channel_id=1, source_target_pairs={{0,20},{4,16},{8,28},{12,24},{16,4},{20,0},{24,12},{28,8},{1,21},{... | collective-permute-start | bytes 49160 | tf_op jit(solution)/shard_map/ppermute | solution.py:190
  14.2 4.2 %collective-permute-start.6 = (f32[4,8,128]{2,1,0:T(8,128)S(1)}, f32[4,8,128]{2,1,0:T(8,128)S(1)}, u32[]{:S(2)}, u32[]{:S(2)}) collective-permute-start(f32[4,8,128]{2,1,0:T(8,128)S(1)} %get-tuple-element.46), channel_id=1, source_target_pairs={{4,24},{8,20},{12,16},{0,28},{20,8},{24,4},{28,0},{16,12},{5,25},{... | collective-permute-start | bytes 49160 | tf_op jit(solution)/shard_map/ppermute | solution.py:190
  21.1 4.8 %collective-permute-start.7 = (f32[20,8,128]{2,1,0:T(8,128)S(1)}, f32[20,8,128]{2,1,0:T(8,128)S(1)}, u32[]{:S(2)}, u32[]{:S(2)}) collective-permute-start(f32[20,8,128]{2,1,0:T(8,128)S(1)} %get-tuple-element.52), channel_id=1, source_target_pairs={{0,16},{16,0},{1,17},{17,1},{2,18},{18,2},{3,19},{19,3},{4,20},{20... | collective-permute-start | bytes 245768 | tf_op jit(solution)/shard_map/ppermute | solution.py:181
  26.6 4.5 %collective-permute-start.8 = (f32[20,8,128]{2,1,0:T(8,128)S(1)}, f32[20,8,128]{2,1,0:T(8,128)S(1)}, u32[]{:S(2)}, u32[]{:S(2)}) collective-permute-start(f32[20,8,128]{2,1,0:T(8,128)S(1)} %get-tuple-element.60), channel_id=1, source_target_pairs={{0,16},{16,0},{1,17},{17,1},{2,18},{18,2},{3,19},{19,3},{4,20},{20... | collective-permute-start | bytes 245768 | tf_op jit(solution)/shard_map/ppermute | solution.py:181
